TPU v7x, 256 devices: a whole 4x4x8 slice. The times are simulated.
256 devices in a mesh: node: 64 (over z, x, core), rep: 4 (over y).
Axes of the slice: x: 4, y: 4, z: 8, core: 2. Of those that a mesh axis runs over, the one named last changes fastest.
Arguments:
- features: bfloat16 [1310720, 256], P('node'), may hold values from -6 to 6
- w_in: bfloat16 [256, 256], replicated, may hold values from -0.375 to 0.375
- w_out: bfloat16 [256, 256], replicated, may hold values from -0.375 to 0.375
- pos_src: int32 [64, 4, 64, 2], P('node', 'rep'), may hold values from 0 to 159
- pos_dst: int32 [64, 4, 64, 2], P('node', 'rep'), may hold values from 0 to 159
- counts: int32 [64, 4, 64], P('node', 'rep'), may hold values from 1 to 2, as said below
- neg_blocks: int32 [64, 2], P('node'), may hold values from 0 to 159
- neg_pick: int32 [64, 4, 64, 2], P('node', 'rep'), may hold values from 0 to 127
Outputs:
- pos_scores: float32 [64, 4, 64, 2, 128], P('node', 'rep')
- neg_term: float32 [64, 4, 64, 2, 128], P('node', 'rep')
- loss: float32 [], replicated
Inputs may be any that keep to these rules, and one draw needn't show every extreme that they name: `counts`: each entry is at most 2; in every draw one owner receives 2 live slots from every device.
All inputs are finite; a program needn't handle non-finite values.
Results may differ from a plain program's by a relative error of at most 0.0027.
Values may be sent and summed in bfloat16 or wider, within the bound.
A program may use at most 192 MiB of HBM per device.

v0:
```python
import jax
import jax.numpy as jnp
from jax import lax
from jax.sharding import Mesh
from jax.sharding import PartitionSpec as P

BLK = 128
NODE = ("node_0", "node_1", "node_2")
NODE_REP = ("node_0", "node_1", "node_2", "rep")


def by_axis(value, axes):
    for axis in axes:
        value = lax.psum(value, axis)
    return value


def encode(rows_in, w_in, w_out):
    hidden = jax.nn.silu(jnp.dot(rows_in, w_in, preferred_element_type=jnp.float32)).astype(
        jnp.bfloat16
    )
    return jnp.dot(hidden, w_out, preferred_element_type=jnp.float32).astype(jnp.bfloat16)


def shards(features, w_in, w_out, pos_src, pos_dst, counts, neg_blocks, neg_pick):
    rows, width = features.shape
    owners = pos_dst.shape[2]
    slots = pos_dst.shape[3]
    embed = encode(features, w_in, w_out)
    blocks = embed.reshape(rows // BLK, BLK, width)
    asked_ids = pos_dst.reshape(owners, slots)
    reply = jnp.take(
        blocks, lax.all_to_all(asked_ids, NODE, split_axis=0, concat_axis=0, tiled=True), axis=0
    )
    fetched = lax.all_to_all(reply, NODE, split_axis=0, concat_axis=0, tiled=True)
    offered = jnp.take(blocks, neg_blocks.reshape(-1), axis=0)
    pool = lax.all_gather(offered, NODE, axis=0, tiled=True)
    source = jnp.take(blocks, pos_src.reshape(-1), axis=0).reshape(owners, slots, BLK, width)
    cand = jnp.take(pool, neg_pick.reshape(-1), axis=0).reshape(owners, slots, BLK, width)
    scale = 1.0 / width**0.5
    raw_pos = (
        jnp.einsum("ocbd,ocbd->ocb", source, fetched, preferred_element_type=jnp.float32) * scale
    )
    scores = jnp.einsum("ocbd,ocsd->ocbs", source, cand, preferred_element_type=jnp.float32) * scale
    live = jnp.arange(slots, dtype=jnp.int32)[None, :] < counts.reshape(owners, 1)
    livex = live[..., None]
    pos_out = jnp.where(livex, raw_pos, 0.0)
    neg_out = jnp.where(livex, jnp.mean(jax.nn.softplus(scores), axis=-1), 0.0)
    pos_loss = jnp.sum(jnp.where(livex, jax.nn.softplus(-raw_pos), 0.0))
    totals = (
        by_axis(pos_loss, NODE_REP),
        by_axis(jnp.sum(neg_out), NODE_REP),
        by_axis(jnp.sum(counts).astype(jnp.float32), NODE_REP),
    )
    loss = (totals[0] + totals[1]) / (BLK * totals[2])
    return (
        pos_out.reshape(1, 1, owners, slots, BLK),
        neg_out.reshape(1, 1, owners, slots, BLK),
        loss,
    )


def solution(mesh):
    finer = Mesh(
        mesh.devices.reshape(8, 4, 2, mesh.shape["rep"]), ("node_0", "node_1", "node_2", "rep")
    )
    return jax.shard_map(
        shards,
        mesh=finer,
        in_specs=(
            P(NODE, None),
            P(),
            P(),
            P(NODE, "rep", None, None),
            P(NODE, "rep", None, None),
            P(NODE, "rep", None),
            P(NODE, None),
            P(NODE, "rep", None, None),
        ),
        out_specs=(P(NODE, "rep", None, None, None), P(NODE, "rep", None, None, None), P()),
        check_vma=False,
    )
```

profile of v0, /device:TPU:1, one launch (start us, length us, event | category | flops | bytes accessed | tf_op | source)
XLA Modules:
  0.0 338.6 jit_solution(679731388551377461)
XLA Ops:
  7.2 0.0 copy-start
  7.2 0.0 all-gather.2.cloned.1.call-start
  7.2 0.7 fusion.9
  7.9 0.7 compare_and_fusion
  8.6 0.0 copy-done
  8.6 0.0 copy-start.2
  8.6 10.9 %convolution_convert_fusion = bf16[20480,256]{1,0:T(8,128)(2,1)} fusion(bf16[256,256]{1,0:T(8,128)(2,1)S(1)} %copy-done, bf16[20480,256]{1,0:T(8,128)(2,1)} %param.8, bf16[256,256]{1,0:T(8,128)(2,1)} %param.9), kind=kOutput, calls=%fused_computation.4 | convolution fusion | flops 5400166400 | bytes 21233664 | tf_op jit(solution)/shard_map/dot_general | solution.py:22
  19.5 4.5 %gather_fusion.2 = bf16[2,128,256]{2,1,0:T(8,128)(2,1)S(1)} fusion(bf16[160,128,256]{2,1,0:T(8,128)(2,1)} %bitcast.40, s32[1024]{0:T(1024)S(1)} %pad_clamp_fusion.1), kind=kCustom, calls=%fused_computation.2 | custom fusion | bytes 262152 | tf_op jit(solution)/shard_map/jit(_take)/gather | solution.py:36
  24.1 0.7 broadcast_select_fusion.3
  24.8 0.0 all-gather.2.cloned.1.call-update
  24.8 0.0 copy-done.2
  24.8 0.1 copy.25
  24.9 22.2 %all_to_all.20 = s32[64,1,2]{2,1,0:T(1,128)S(1)} all-to-all(s32[64,1,2]{2,1,0:T(1,128)S(1)} %copy.25), channel_id=1, replica_groups=mesh['node_0'=8,'node_1'=4,'node_2'=2,'rep'=4] {'node_0','node_1','node_2'}, dimensions={0} | all-to-all | bytes 1024 | tf_op jit(solution)/shard_map/all_to_all | solution.py:33
  47.1 0.1 copy.26
  47.2 0.1 copy.27
  47.3 0.1 copy.29
  47.4 0.1 reshape.231
  47.6 10.7 %gather_fusion.1 = bf16[128,128,256]{2,1,0:T(8,128)(2,1)} fusion(bf16[160,128,256]{2,1,0:T(8,128)(2,1)} %bitcast.41, s32[1024]{0:T(1024)S(1)} %pad_clamp_fusion.2), kind=kCustom, calls=%fused_computation.1 | custom fusion | bytes 16777728 | tf_op jit(solution)/shard_map/jit(_take)/gather | solution.py:32
  58.3 7.6 %broadcast_select_fusion = bf16[64,2,128,256]{3,2,1,0:T(8,128)(2,1)} fusion(bf16[64,2,128,256]{3,2,1,0:T(8,128)(2,1)} %bitcast.39, pred[64,2]{1,0:T(8,128)(4,1)S(1)} %copy.27), kind=kLoop, calls=%fused_computation.14 | loop fusion | flops 4194304 | bytes 16777344 | tf_op jit(solution)/shard_map/jit(_take)/select_n | solution.py:32
  65.8 0.0 copy-start.5
  65.8 0.0 copy-start.3
  65.9 0.0 copy-start.4
  65.9 5.9 %all-to-all-start.1 = ((bf16[64,2,128,256]{3,2,1,0:T(8,128)(2,1)}), bf16[64,2,128,256]{3,2,1,0:T(8,128)(2,1)}, u32[]{:S(2)}, u32[]{:S(2)}) async-start(bf16[64,2,128,256]{3,2,1,0:T(8,128)(2,1)} %broadcast_select_fusion), calls=%async_computation.1 | async-start | bytes 16777216 | tf_op jit(solution)/shard_map/all_to_all | solution.py:35
  71.8 0.0 copy-done.5
  71.8 0.6 reduce_sum.39
  73.0 0.0 copy-done.3
  73.1 0.1 copy.24
  73.2 0.1 copy.23
  73.3 0.0 copy-done.4
  73.3 0.1 copy.31
  73.4 0.1 copy.30
  73.5 0.1 reshape.215
  73.6 0.1 reshape.220
  73.8 10.6 %gather_fusion = bf16[128,128,256]{2,1,0:T(8,128)(2,1)} fusion(bf16[160,128,256]{2,1,0:T(8,128)(2,1)} %bitcast.42, s32[1024]{0:T(1024)S(1)} %pad_clamp_fusion.3), kind=kCustom, calls=%fused_computation | custom fusion | bytes 16777728 | tf_op jit(solution)/shard_map/jit(_take)/gather | solution.py:38
  84.4 0.1 iota_compare_fusion
  84.5 72.6 %all-gather.2.cloned.1.call-done = bf16[128,128,256]{2,1,0:T(8,128)(2,1)} async-done(((bf16[2,128,256]{2,1,0:T(8,128)(2,1)}), bf16[128,128,256]{2,1,0:T(8,128)(2,1)}) %all-gather.2.cloned.1.call-update) | async-done | bytes 8388624 | tf_op jit(solution)/shard_map/all_gather | solution.py:37
  157.1 10.0 %gather_fusion.3 = bf16[128,128,256]{2,1,0:T(8,128)(2,1)} fusion(bf16[128,128,256]{2,1,0:T(8,128)(2,1)} %all-gather.2.cloned.1.call-done, s32[1024]{0:T(1024)S(1)} %pad_clamp_fusion), kind=kCustom, calls=%fused_computation.3 | custom fusion | bytes 16777728 | tf_op jit(solution)/shard_map/jit(_take)/gather | solution.py:39
  167.0 9.9 %fusion.5 = (u8[64,128,128]{1,2,0:T(8,128)(4,1)S(1)}, f32[64,2,128,128]{2,3,1,0:T(8,128)}) fusion(bf16[64,2,128,256]{3,2,1,0:T(8,128)(2,1)} %bitcast.43, pred[64,2]{1,0:T(8,128)(4,1)S(1)} %copy.30, bf16[64,2,128,256]{3,2,1,0:T(8,128)(2,1)} %bitcast.37, pred[64,2]{1,0:T(8,128)(4,1)S(1)} %copy.23), kind=kOutput, calls=%fused_computation.17 | convolution fusion | flops 1093664768 | bytes 26214656 | tf_op jit(solution)/shard_map/ocbd,ocsd->ocbs/dot_general | solution.py:44
  176.9 0.0 copy-start.1
  177.0 8.5 %select_reduce_fusion = f32[64,2,128]{2,1,0:T(2,128)S(1)} fusion(f32[64,2,128,128]{2,3,1,0:T(8,128)} %get-tuple-element.15, u8[64,128,128]{1,2,0:T(8,128)(4,1)S(1)} %get-tuple-element.14), kind=kLoop, calls=%fused_computation.10 | loop fusion | flops 23052288 | bytes 9502720 | tf_op jit(solution)/shard_map/reduce_sum | solution.py:48
  185.5 88.5 %all-to-all-done.1 = bf16[64,2,128,256]{3,2,1,0:T(8,128)(2,1)} async-done(((bf16[64,2,128,256]{3,2,1,0:T(8,128)(2,1)}), bf16[64,2,128,256]{3,2,1,0:T(8,128)(2,1)}, u32[]{:S(2)}, u32[]{:S(2)}) %all-to-all-start.1) | async-done | bytes 8388640 | tf_op jit(solution)/shard_map/all_to_all | solution.py:35
  274.0 8.8 %fusion = f32[64,2,128]{2,1,0:T(2,128)S(1)} fusion(bf16[64,2,128,256]{3,2,1,0:T(8,128)(2,1)} %all-to-all-done.1, bf16[64,2,128,256]{3,2,1,0:T(8,128)(2,1)} %bitcast.38, pred[64,2]{1,0:T(8,128)(4,1)S(1)} %copy.23), kind=kLoop, calls=%fused_computation.7 | loop fusion | flops 20955136 | bytes 16842880 | tf_op jit(solution)/shard_map/ocbd,ocbd->ocb/dot_general | solution.py:42
  282.8 1.5 select_reduce_fusion.1
  285.6 0.8 bitcast_select_fusion
  286.3 15.0 %all-reduce = (f32[]{:T(128)}, f32[]{:T(128)}) all-reduce(f32[]{:T(128)S(6)} %add.133, f32[]{:T(128)S(6)} %convert_element_type.11), channel_id=1, replica_groups=mesh['node_0'=8,'node_1'=4,'node_2'=2,'rep'=4] {'node_0'}, use_global_device_ids=true, to_apply=%region_2.3 | all-reduce | flops 2 | bytes 16 | tf_op jit(solution)/shard_map/psum | solution.py:14
  301.4 9.6 %all-reduce.2 = (f32[]{:T(128)}, f32[]{:T(128)}) all-reduce(f32[]{:T(128)} %get-tuple-element.5, f32[]{:T(128)} %get-tuple-element.6), channel_id=1, replica_groups=mesh['node_0'=8,'node_1'=4,'node_2'=2,'rep'=4] {'node_1'}, use_global_device_ids=true, to_apply=%region_3.4 | all-reduce | flops 2 | bytes 16 | tf_op jit(solution)/shard_map/psum | solution.py:14
  310.9 8.9 %all-reduce.3 = (f32[]{:T(128)}, f32[]{:T(128)}) all-reduce(f32[]{:T(128)} %get-tuple-element.9, f32[]{:T(128)} %get-tuple-element.10), channel_id=1, replica_groups=mesh['node_0'=8,'node_1'=4,'node_2'=2,'rep'=4] {'node_2'}, use_global_device_ids=true, to_apply=%region_4.5 | all-reduce | flops 2 | bytes 16 | tf_op jit(solution)/shard_map/psum | solution.py:14
  319.9 9.4 %all-reduce.1 = (f32[]{:T(128)}, f32[]{:T(128)}) all-reduce(f32[]{:T(128)} %get-tuple-element.11, f32[]{:T(128)} %get-tuple-element.12), channel_id=1, replica_groups=mesh['node_0'=8,'node_1'=4,'node_2'=2,'rep'=4] {'rep'}, use_global_device_ids=true, to_apply=%region_5.6 | all-reduce | flops 2 | bytes 16 | tf_op jit(solution)/shard_map/psum | solution.py:14
  330.6 0.0 copy-done.1
  (10 shorter events, 0.1 us)
Async XLA Ops:
  7.2 1.4 copy-start
  7.2 149.9 %all-gather.2.cloned.1.call-start = ((), (), s32[]{:S(2)}) async-start(), calls=%async_computation.2 | async-start | bytes 8519680 | tf_op jit(solution)/shard_map/all_gather | solution.py:37
  8.6 16.2 %copy-start.2 = (s32[1,1,64,2]{2,3,1,0:T(2,128)S(1)}, s32[1,1,64,2]{2,3,1,0:T(2,128)}, u32[]{:S(2)}) copy-start(s32[1,1,64,2]{2,3,1,0:T(2,128)} %param.12) | copy-start | bytes 1540
  65.8 5.9 %copy-start.5 = (s32[1,1,64]{2,1,0:T(1,128)S(1)}, s32[1,1,64]{2,1,0:T(1,128)}, u32[]{:S(2)}) copy-start(s32[1,1,64]{2,1,0:T(1,128)} %param.13) | copy-start | bytes 772
  65.8 7.2 %copy-start.3 = (s32[1,1,64,2]{2,3,1,0:T(2,128)S(1)}, s32[1,1,64,2]{2,3,1,0:T(2,128)}, u32[]{:S(2)}) copy-start(s32[1,1,64,2]{2,3,1,0:T(2,128)} %param.11) | copy-start | bytes 1540
  65.9 7.4 %copy-start.4 = (s32[1,1,64,2]{2,3,1,0:T(2,128)S(1)}, s32[1,1,64,2]{2,3,1,0:T(2,128)}, u32[]{:S(2)}) copy-start(s32[1,1,64,2]{2,3,1,0:T(2,128)} %param.15) | copy-start | bytes 1540
  65.9 208.1 %all-to-all-start.1 = ((bf16[64,2,128,256]{3,2,1,0:T(8,128)(2,1)}), bf16[64,2,128,256]{3,2,1,0:T(8,128)(2,1)}, u32[]{:S(2)}, u32[]{:S(2)}) async-start(bf16[64,2,128,256]{3,2,1,0:T(8,128)(2,1)} %broadcast_select_fusion), calls=%async_computation.1 | async-start | bytes 16777216 | tf_op jit(solution)/shard_map/all_to_all | solution.py:35
  176.9 153.7 %copy-start.1 = (bf16[256,256]{1,0:T(8,128)(2,1)S(1)}, bf16[256,256]{1,0:T(8,128)(2,1)}, u32[]{:S(2)}) copy-start(bf16[256,256]{1,0:T(8,128)(2,1)} %param.10) | copy-start | bytes 393220
Sparse Core Ops, SparseCore 0:
  24.9 132.0 all-gather.1
where the time goes:
time: 339 us
  waiting for transfers between devices  161 us (47%)
  blocking collectives  65.1 us (19%)
  local copies, waits for them, and re-layouts  37.1 us (11%)
  other arithmetic  30 us (9%)
  matrix products  20.8 us (6%)
  between operations  18.6 us (5%)
  starting transfers between devices  5.93 us (2%)
    all_to_all x1, waiting for transfers between devices, shards(): lax.all_to_all(reply, NODE, split_axis=0, concat_axis=0, tiled=True)  88.5 us
    all_gather x1, waiting for transfers between devices, shards(): pool = lax.all_gather(offered, NODE, axis=0, tiled=True)  72.6 us
    psum x4, blocking collectives, by_axis(): value = lax.psum(value, axis)  42.9 us
    all_to_all x1, blocking collectives, shards(): lax.all_to_all(asked_ids, NODE, split_axis=0, concat_axis=0, tiled=True)  22.2 us
    dot_general x1, matrix products, encode(): jnp.dot(hidden, w_out, preferred_element_type=jnp.float32)  10.9 us
    gather x1, local copies, waits for them, and re-layouts, shards(): jnp.take(blocks, lax.all_to_all(asked_ids, NODE, split_axis=0, concat_axi...  10.7 us
    gather x1, local copies, waits for them, and re-layouts, shards(): jnp.take(blocks, pos_src.reshape(-1), axis=0)  10.6 us
    gather x1, local copies, waits for them, and re-layouts, shards(): jnp.take(pool, neg_pick.reshape(-1), axis=0)  9.96 us
  transfers between devices with their start and end apart: 2, of which 2 were waited for; matrix products, arithmetic and copies ran while one was open for 18% of the time, Pallas kernels for 0%

commit v1 on v0

v1 whole, which is shorter than its diff:
```python
import functools

import jax
import jax.numpy as jnp
from jax import lax
from jax.experimental import pallas as pl
from jax.experimental.pallas import tpu as pltpu
from jax.sharding import PartitionSpec as P

BLK = 128
ALL = ("node", "rep")
VMEM = pl.BlockSpec(memory_space=pltpu.VMEM)
SMEM = pl.BlockSpec(memory_space=pltpu.SMEM)


def silu(v):
    return v / (1.0 + jnp.exp(-v))


def encode(rows_in, w_in, w_out):
    hidden = jax.nn.silu(jnp.dot(rows_in, w_in, preferred_element_type=jnp.float32)).astype(
        jnp.bfloat16
    )
    return jnp.dot(hidden, w_out, preferred_element_type=jnp.float32).astype(jnp.bfloat16)


def rows_kernel(part_ref, x_ref, w_in_ref, w_out_ref, out_ref):
    group, rows, width = x_ref.shape
    x = x_ref[...].reshape(group * rows, width)
    h = jnp.dot(x, w_in_ref[...], preferred_element_type=jnp.float32)
    h = silu(h).astype(jnp.bfloat16)
    e = jnp.dot(h, w_out_ref[...], preferred_element_type=jnp.float32).astype(jnp.bfloat16)
    n = group * rows
    i = lax.broadcasted_iota(jnp.int32, (n, n), 0)
    j = lax.broadcasted_iota(jnp.int32, (n, n), 1)
    perm = jnp.where(j == (i % group) * rows + i // group, 1.0, 0.0).astype(jnp.bfloat16)
    t = jnp.dot(perm, e, preferred_element_type=jnp.float32).astype(jnp.bfloat16)
    half = width // 2
    out_ref[:, 0] = t[:, :half].reshape(rows, group, half)
    out_ref[:, 1] = t[:, half:].reshape(rows, group, half)


def rows_of_blocks(features, w_in, w_out, parts, group=16):
    total, width = features.shape
    blocks = total // BLK
    rows = BLK // parts
    part = lax.axis_index("rep").astype(jnp.int32).reshape(1)
    return pl.pallas_call(
        rows_kernel,
        grid_spec=pltpu.PrefetchScalarGridSpec(
            num_scalar_prefetch=1,
            grid=(blocks // group,),
            in_specs=[
                pl.BlockSpec((group, rows, width), lambda g, p: (g, p[0], 0)),
                pl.BlockSpec((width, width), lambda g, p: (0, 0)),
                pl.BlockSpec((width, width), lambda g, p: (0, 0)),
            ],
            out_specs=pl.BlockSpec((rows, 2, group, width // 2), lambda g, p: (0, 0, g, 0)),
        ),
        out_shape=jax.ShapeDtypeStruct((rows, 2, blocks, width // 2), jnp.bfloat16),
        cost_estimate=pl.CostEstimate(
            flops=2 * blocks * rows * width * (2 * width + group * rows),
            bytes_accessed=4 * blocks * rows * width,
            transcendentals=blocks * rows * width,
        ),
        name="rows",
    )(part, features.reshape(blocks, BLK, width), w_in, w_out)


def hub_kernel(scale, rows_ref, src_ref, dst_ref, out_ref, ends_ref):
    nodes, blocks, width = rows_ref.shape
    edges = src_ref.shape[1]
    lane = lax.broadcasted_iota(jnp.int32, (edges, blocks), 1)
    per = edges // nodes

    def pick(ids, node):
        hot = jnp.where(ids == lane, 1.0, 0.0).astype(jnp.bfloat16)
        return jnp.dot(hot, rows_ref[node], preferred_element_type=jnp.float32)

    def ends(g, _):
        for k in range(8):
            node = g * 8 + k
            got = pick(dst_ref[g, :, k : k + 1], node)
            ends_ref[node] = got.reshape(nodes, per, width)
        return 0

    lax.fori_loop(0, nodes // 8, ends, 0)
    place = lax.broadcasted_iota(jnp.int32, (nodes, per, nodes), 0)
    at = lax.broadcasted_iota(jnp.int32, (nodes, per, nodes), 2)
    keep = place == at

    def dots(g, _):
        for k in range(8):
            node = g * 8 + k
            got = pick(src_ref[g, :, k : k + 1], node).reshape(nodes, per, width)
            sums = jnp.sum(got * ends_ref[:, node], axis=2, keepdims=True)
            out_ref[node] = jnp.sum(jnp.where(keep, sums, 0.0), axis=0) * scale
        return 0

    lax.fori_loop(0, nodes // 8, dots, 0)


def hub(rows, src_ids, dst_ids, scale):
    nodes, blocks, width = rows.shape
    edges = src_ids.shape[1]
    per = edges // nodes
    return pl.pallas_call(
        functools.partial(hub_kernel, scale),
        in_specs=[VMEM] * 3,
        out_specs=VMEM,
        out_shape=jax.ShapeDtypeStruct((nodes, per, nodes), jnp.float32),
        scratch_shapes=[pltpu.VMEM((nodes, nodes, per, width), jnp.float32)],
        compiler_params=pltpu.CompilerParams(vmem_limit_bytes=48 * 2**20),
        cost_estimate=pl.CostEstimate(
            flops=4 * nodes * edges * blocks * width, bytes_accessed=8 * 2**20, transcendentals=0
        ),
        name="hub",
    )(rows, src_ids, dst_ids)


def neg_kernel(scale, embed_ref, pool_ref, src_ref, pick_ref, out_ref):
    slots = out_ref.shape[0]
    rows = pool_ref.shape[1]

    def step(j, _):
        score = lax.dot_general(
            pool_ref[pick_ref[j]],
            embed_ref[src_ref[j]],
            (((1,), (1,)), ((), ())),
            preferred_element_type=jnp.float32,
        )
        v = score * scale
        soft = jnp.maximum(v, 0.0) + jnp.log1p(jnp.exp(-jnp.abs(v)))
        out_ref[pl.ds(j, 1), :] = jnp.sum(soft, axis=0, keepdims=True) * (1.0 / rows)
        return 0

    lax.fori_loop(0, slots, step, 0)


def neg_means(embed, pool, src, pick, scale):
    slots = src.shape[0]
    width = pool.shape[2]
    return pl.pallas_call(
        functools.partial(neg_kernel, scale),
        in_specs=[VMEM, VMEM, SMEM, SMEM],
        out_specs=VMEM,
        out_shape=jax.ShapeDtypeStruct((slots, BLK), jnp.float32),
        compiler_params=pltpu.CompilerParams(vmem_limit_bytes=32 * 2**20),
        cost_estimate=pl.CostEstimate(
            flops=slots * 2 * BLK * BLK * width,
            bytes_accessed=20 * 2**20,
            transcendentals=2 * slots * BLK * BLK,
        ),
        name="neg",
    )(embed, pool, src, pick)


def shards(nodes, reps, features, w_in, w_out, pos_src, pos_dst, counts, neg_blocks, neg_pick):
    total, width = features.shape
    blocks = total // BLK
    slots = pos_dst.shape[3]
    scale = 1.0 / width**0.5
    offered = jnp.concatenate(
        [
            lax.dynamic_slice_in_dim(features, neg_blocks[0, k] * BLK, BLK, 0)
            for k in range(neg_blocks.shape[1])
        ]
    )
    pool = lax.all_gather(
        encode(offered, w_in, w_out).reshape(-1, BLK, width), "node", axis=0, tiled=True
    )
    sent = rows_of_blocks(features, w_in, w_out, reps).reshape(nodes, blocks, width // 2)
    mine = lax.all_to_all(sent, "node", split_axis=0, concat_axis=0, tiled=True)

    own = jnp.stack([pos_src.reshape(nodes, slots), pos_dst.reshape(nodes, slots)])
    ids = lax.all_gather(own, ALL, axis=0, tiled=False).reshape(nodes, reps, 2, nodes, slots)

    def columns(t):
        t = t.reshape(nodes // 8, 8, nodes * reps * slots)
        return jnp.swapaxes(t, 1, 2)

    src_ids = columns(jnp.transpose(ids[:, :, 0], (0, 2, 1, 3)))
    dst_ids = columns(jnp.transpose(ids[:, :, 1], (2, 0, 1, 3)))

    embed = encode(features, w_in, w_out).reshape(blocks, BLK, width)
    neg = neg_means(embed, pool, pos_src.reshape(-1), neg_pick.reshape(-1), scale)

    part = hub(mine, src_ids, dst_ids, scale)
    back = lax.all_to_all(
        part.reshape(nodes * reps, slots * nodes), ALL, split_axis=0, concat_axis=0, tiled=True
    )
    back = back.reshape(nodes // 2, 2, reps, slots, nodes).sum(axis=1)
    raw = jnp.transpose(back, (3, 2, 1, 0)).reshape(nodes, slots, BLK)

    live = jnp.arange(slots, dtype=jnp.int32)[None, :] < counts.reshape(nodes, 1)
    livex = live[..., None]
    pos_out = jnp.where(livex, raw, 0.0)
    neg_out = jnp.where(livex, neg.reshape(nodes, slots, BLK), 0.0)
    partial = jnp.sum(jnp.where(livex, jax.nn.softplus(-raw), 0.0)) + jnp.sum(neg_out)
    sums = lax.psum(jnp.stack([partial, jnp.sum(counts).astype(jnp.float32)]), ALL)
    loss = sums[0] / (BLK * sums[1])
    return (
        pos_out.reshape(1, 1, nodes, slots, BLK),
        neg_out.reshape(1, 1, nodes, slots, BLK),
        loss,
    )


def solution(mesh):
    n, r = mesh.shape["node"], mesh.shape["rep"]
    return jax.shard_map(
        functools.partial(shards, n, r),
        mesh=mesh,
        in_specs=(
            P("node", None),
            P(),
            P(),
            P("node", "rep", None, None),
            P("node", "rep", None, None),
            P("node", "rep", None),
            P("node", None),
            P("node", "rep", None, None),
        ),
        out_specs=(P("node", "rep", None, None, None), P("node", "rep", None, None, None), P()),
        check_vma=False,
    )
```

time: 339 us -> 367 us (1.083)
  waiting for transfers between devices: 161 us -> 0.02 us
  blocking collectives: 65.1 us -> 215 us
  Pallas kernels: 0 us -> 65.1 us
  other arithmetic: 30 us -> 3.65 us
  starting transfers between devices: 5.93 us -> 25.1 us
  local copies, waits for them, and re-layouts: 37.1 us -> 24.3 us
  matrix products: 20.8 us -> 12.8 us
    all_gather x0 -> x1, blocking collectives: none -> 136 us  [shards(): lax.all_gather(own, ALL, axis=0, tiled=False)]
    all_to_all x1 -> x2, waiting for transfers between devices: 88.5 us -> 0.01 us  [the longest x1 0.01 us: shards(): lax.all_to_all(part.reshape(nodes * reps, slots * nodes), ALL, split_axis...]
    all_gather x1, waiting for transfers between devices: 72.6 us -> 0.01 us  [shards(): lax.all_gather(encode(offered, w_in, w_out).reshape(-1, BLK, width), 'nod...]
    pallas_call x0 -> x3, Pallas kernels: none -> 65.1 us  [the longest x1 27.5 us: neg_means(): pl.pallas_call(functools.partial(neg_kernel, scale), in_specs=[VMEM, VMEM...]
    psum x4 -> x1, blocking collectives: 42.9 us -> 79.1 us  [shards(): lax.psum(jnp.stack([partial, jnp.sum(counts).astype(jnp.float32)]), ALL)]
    gather x4 -> x0, local copies, waits for them, and re-layouts: 35.8 us -> none  [the longest x1 10.7 us: shards(): jnp.take(blocks, lax.all_to_all(asked_ids, NODE, split_axis=0, concat_axi...]
    all_to_all x1 -> x0, blocking collectives: 22.2 us -> none  [shards(): lax.all_to_all(asked_ids, NODE, split_axis=0, concat_axis=0, tiled=True)]
    all_to_all x1 -> x2, starting transfers between devices: 5.89 us -> 25 us  [the longest x1 13.1 us: shards(): mine = lax.all_to_all(sent, 'node', split_axis=0, concat_axis=0, tiled=True)]
  transfers between devices with their start and end apart: 2 -> 3, of which waited for: 2 -> 0; matrix products, arithmetic and copies ran while one was open for 18% -> 7% of each run, Pallas kernels for 0% -> 10%
where the time goes in v1:
time: 367 us; the launch traced here: 366 us
  blocking collectives  215 us (59%)
  Pallas kernels  65.1 us (18%)
  starting transfers between devices  25.1 us (7%)
  local copies, waits for them, and re-layouts  24.3 us (7%)
  between operations  19.9 us (5%)
  matrix products  12.8 us (3%)
    all_gather x1, blocking collectives, shards(): lax.all_gather(own, ALL, axis=0, tiled=False)  136 us
    psum x1, blocking collectives, shards(): lax.psum(jnp.stack([partial, jnp.sum(counts).astype(jnp.float32)]), ALL)  79.1 us
    pallas_call x1, Pallas kernels, neg_means(): pl.pallas_call(functools.partial(neg_kernel, scale), in_specs=[VMEM, VMEM...  27.5 us
    pallas_call x1, Pallas kernels, hub(): pl.pallas_call(functools.partial(hub_kernel, scale), in_specs=[VMEM] * 3,...  27 us
    all_to_all x1, starting transfers between devices, shards(): mine = lax.all_to_all(sent, 'node', split_axis=0, concat_axis=0, tiled=True)  13.1 us
    dot_general x2, matrix products, encode(): jnp.dot(hidden, w_out, preferred_element_type=jnp.float32)  12.8 us
    all_to_all x1, starting transfers between devices, shards(): lax.all_to_all(part.reshape(nodes * reps, slots * nodes), ALL, split_axis...  11.9 us
    unnamed x23, local copies, waits for them, and re-layouts  10.8 us
  transfers between devices with their start and end apart: 3, of which 0 were waited for; matrix products, arithmetic and copies ran while one was open for 7% of the time, Pallas kernels for 10%

profile of v1, /device:TPU:1, one launch (start us, length us, event | category | flops | bytes accessed | tf_op | source)
XLA Modules:
  0.0 366.1 jit_solution(2281541844166676216)
XLA Ops:
  7.2 0.0 copy-start.5
  7.2 0.0 copy-start.7
  7.2 0.0 all-gather.3.cloned.1.call-start
  7.2 1.3 fusion.18
  9.9 0.9 constant_dynamic-slice_fusion.1
  10.7 2.0 convolution_convert_fusion.1
  12.7 0.0 all-gather.3.cloned.1.call-update
  12.7 10.6 %rows.1 = bf16[32,2,160,128]{3,2,1,0:T(8,128)(2,1)} custom-call(s32[1]{0:T(128)} %bitcast.1.part_ref, bf16[160,128,256]{2,1,0:T(8,128)(2,1)} %bitcast.47, bf16[256,256]{1,0:T(8,128)(2,1)} %w_in_ref.1, bf16[256,256]{1,0:T(8,128)(2,1)} %w_out_ref.1), custom_call_target="tpu_custom_call" | custom-call | flops 2684354560 | bytes 5242880 | tf_op jit(solution)/shard_map/rows/pallas_call | solution.py:48
  23.4 13.1 %all-to-all-start = ((bf16[64,160,128]{2,1,0:T(8,128)(2,1)}), bf16[64,160,128]{2,1,0:T(8,128)(2,1)}, u32[]{:S(2)}, u32[]{:S(2)}) async-start(bf16[64,160,128]{2,1,0:T(8,128)(2,1)} %bitcast.48), calls=%async_computation | async-start | bytes 5242880 | tf_op jit(solution)/shard_map/all_to_all | solution.py:173
  36.5 0.0 copy-done.5
  36.5 0.0 copy-done.7
  36.6 136.1 %all-gather = s32[512,64,2]{1,2,0:T(2,128)S(1)} all-gather(s32[2,64,2]{1,2,0:T(2,128)S(1)} %pad_add_fusion), channel_id=2, replica_groups=mesh['node'=64,'rep'=4] {'node','rep'}, dimensions={0}, use_global_device_ids=true | all-gather | bytes 263168 | tf_op jit(solution)/shard_map/all_gather | solution.py:176
  172.6 0.2 slice_bitcast_fusion
  172.8 0.2 copy.37
  173.0 2.1 reshape.114
  175.1 0.0 copy-start.3
  175.1 0.0 copy-start.4
  175.1 2.1 reshape.115
  177.2 4.3 %copy_bitcast_fusion = (s32[8,512,8]{2,1,0:T(8,128)S(1)}, s32[8,512,8]{2,1,0:T(8,128)}) fusion(s32[8,8,512]{1,0,2:T(8,128)} %reshape.115, s32[8,8,512]{1,0,2:T(8,128)} %reshape.114), kind=kLoop, calls=%fused_computation.2 | loop fusion | bytes 524288 | tf_op jit(solution)/shard_map/transpose | solution.py:180
  181.5 0.0 all-to-all-done.rows_ref
  181.5 0.0 copy-start.2
  181.5 1.6 copy-done.2
  183.1 27.0 %hub.1 = f32[64,8,64]{2,1,0:T(8,128)S(1)} custom-call(bf16[64,160,128]{2,1,0:T(8,128)(2,1)} %all-to-all-done.rows_ref, s32[8,512,8]{2,1,0:T(8,128)S(1)} %copy-done.2, s32[8,512,8]{2,1,0:T(8,128)S(1)} %get-tuple-element.19.dst_ref), custom_call_target="tpu_custom_call" | custom-call | flops 2684354560 | bytes 8388608 | tf_op jit(solution)/shard_map/hub/pallas_call | solution.py:107
  210.1 0.7 all_to_all.10
  210.9 11.9 %all-to-all-start.1 = ((f32[256,1,128]{2,1,0:T(1,128)}), f32[256,1,128]{2,1,0:T(1,128)S(1)}, u32[]{:S(2)}, u32[]{:S(2)}) async-start(f32[256,1,128]{2,1,0:T(1,128)} %bitcast.13), calls=%async_computation.1 | async-start | bytes 262144 | tf_op jit(solution)/shard_map/all_to_all | solution.py:189
  222.8 0.0 copy-done.3
  222.8 0.0 copy-done.4
  222.8 0.0 copy-start.8
  222.8 0.0 copy-start.6
  222.8 10.8 %convolution_convert_fusion = bf16[20480,256]{1,0:T(8,128)(2,1)} fusion(bf16[256,256]{1,0:T(8,128)(2,1)S(1)} %copy-done.3, bf16[20480,256]{1,0:T(8,128)(2,1)} %param.8, bf16[256,256]{1,0:T(8,128)(2,1)S(1)} %copy-done.4), kind=kOutput, calls=%fused_computation | convolution fusion | flops 5400166400 | bytes 21233664 | tf_op jit(solution)/shard_map/dot_general | solution.py:24
  233.7 0.1 copy.31
  233.8 0.0 copy-done.8
  233.8 0.1 iota_compare_fusion
  233.9 0.2 lt.35
  234.0 0.1 copy.24
  234.1 0.6 reduce_sum.39
  234.7 0.1 reshape.120.src_ref
  234.9 0.0 copy-done.6
  234.9 0.1 copy.32
  235.0 0.1 reshape.121.pick_ref
  235.8 0.0 all-to-all-done.1
  235.8 0.5 broadcast.55
  236.3 1.0 reduce.5
  237.3 0.2 reshape.116
  237.5 0.2 reduce_sum.36
  237.7 1.0 fusion.12
  238.6 0.0 all-gather.3.cloned.1.call-done.pool_ref
  238.6 0.0 copy-start
  238.6 4.0 %copy-done = bf16[20480,256]{1,0:T(8,128)(2,1)S(1)} copy-done((bf16[20480,256]{1,0:T(8,128)(2,1)S(1)}, bf16[20480,256]{1,0:T(8,128)(2,1)}, u32[]{:S(2)}) %copy-start) | copy-done | bytes 10485784
  242.6 0.0 copy-start.1
  242.6 3.4 copy-done.1
  246.0 27.5 %neg.32 = f32[128,128]{1,0:T(8,128)S(1)} custom-call(bf16[160,128,256]{2,1,0:T(8,128)(2,1)S(1)} %bitcast.45, bf16[128,128,256]{2,1,0:T(8,128)(2,1)S(1)} %copy-done.1, s32[128]{0:T(128)S(1)} %reshape.120.src_ref, s32[128]{0:T(128)S(1)} %reshape.121.pick_ref), custom_call_target="tpu_custom_call" | custom-call | flops 1073741824 | bytes 20971520 | tf_op jit(solution)/shard_map/neg/pallas_call | solution.py:143
  273.5 0.7 select_reduce_fusion
  275.5 0.1 pad_maximum_fusion
  275.6 79.1 %psum.7 = f32[2]{0:T(128)S(1)} all-reduce(f32[2]{0:T(128)S(1)} %pad_maximum_fusion), channel_id=1, replica_groups=mesh['node'=64,'rep'=4] {'node','rep'}, use_global_device_ids=true, to_apply=%region_4.5 | all-reduce | flops 2 | bytes 16 | tf_op jit(solution)/shard_map/psum | solution.py:200
  354.7 0.6 fusion.17
  355.3 0.1 copy.33
  355.4 0.7 copy.35
  356.1 0.7 copy.36
  (3 shorter events, 0.1 us)
Async XLA Ops:
  7.2 29.4 %copy-start.5 = (s32[1,1,64,2]{2,3,1,0:T(2,128)S(1)}, s32[1,1,64,2]{2,3,1,0:T(2,128)}, u32[]{:S(2)}) copy-start(s32[1,1,64,2]{2,3,1,0:T(2,128)} %param.11) | copy-start | bytes 1540
  7.2 29.4 %copy-start.7 = (s32[1,1,64,2]{2,3,1,0:T(2,128)S(1)}, s32[1,1,64,2]{2,3,1,0:T(2,128)}, u32[]{:S(2)}) copy-start(s32[1,1,64,2]{2,3,1,0:T(2,128)} %param.12) | copy-start | bytes 1540
  7.2 231.5 %all-gather.3.cloned.1.call-start = ((), (), s32[]{:S(2)}) async-start(), calls=%async_computation.2 | async-start | bytes 8519680 | tf_op jit(solution)/shard_map/all_gather | solution.py:169
  23.4 158.2 %all-to-all-start = ((bf16[64,160,128]{2,1,0:T(8,128)(2,1)}), bf16[64,160,128]{2,1,0:T(8,128)(2,1)}, u32[]{:S(2)}, u32[]{:S(2)}) async-start(bf16[64,160,128]{2,1,0:T(8,128)(2,1)} %bitcast.48), calls=%async_computation | async-start | bytes 5242880 | tf_op jit(solution)/shard_map/all_to_all | solution.py:173
  175.1 47.7 %copy-start.3 = (bf16[256,256]{1,0:T(8,128)(2,1)S(1)}, bf16[256,256]{1,0:T(8,128)(2,1)}, u32[]{:S(2)}) copy-start(bf16[256,256]{1,0:T(8,128)(2,1)} %w_out_ref.1) | copy-start | bytes 393220
  175.1 47.7 %copy-start.4 = (bf16[256,256]{1,0:T(8,128)(2,1)S(1)}, bf16[256,256]{1,0:T(8,128)(2,1)}, u32[]{:S(2)}) copy-start(bf16[256,256]{1,0:T(8,128)(2,1)} %w_in_ref.1) | copy-start | bytes 393220
  181.5 1.6 copy-start.2
  210.9 24.9 %all-to-all-start.1 = ((f32[256,1,128]{2,1,0:T(1,128)}), f32[256,1,128]{2,1,0:T(1,128)S(1)}, u32[]{:S(2)}, u32[]{:S(2)}) async-start(f32[256,1,128]{2,1,0:T(1,128)} %bitcast.13), calls=%async_computation.1 | async-start | bytes 262144 | tf_op jit(solution)/shard_map/all_to_all | solution.py:189
  222.8 11.0 %copy-start.8 = (s32[1,1,64]{2,1,0:T(1,128)S(1)}, s32[1,1,64]{2,1,0:T(1,128)}, u32[]{:S(2)}) copy-start(s32[1,1,64]{2,1,0:T(1,128)} %param.13) | copy-start | bytes 772
  222.8 12.0 %copy-start.6 = (s32[1,1,64,2]{2,3,1,0:T(2,128)S(1)}, s32[1,1,64,2]{2,3,1,0:T(2,128)}, u32[]{:S(2)}) copy-start(s32[1,1,64,2]{2,3,1,0:T(2,128)} %param.15) | copy-start | bytes 1540
  238.6 4.0 %copy-start = (bf16[20480,256]{1,0:T(8,128)(2,1)S(1)}, bf16[20480,256]{1,0:T(8,128)(2,1)}, u32[]{:S(2)}) copy-start(bf16[20480,256]{1,0:T(8,128)(2,1)} %convolution_convert_fusion) | copy-start | bytes 31457284
  242.6 3.4 copy-start.1
Sparse Core Ops, SparseCore 0:
  12.9 110.3 all-gather.2

commit v2 on v0

v2 whole, which is shorter than its diff:
```python
import functools

import jax
import jax.numpy as jnp
from jax import lax
from jax.experimental import pallas as pl
from jax.experimental.pallas import tpu as pltpu
from jax.sharding import PartitionSpec as P

MESH = pl.DeviceIdType.MESH
VMEM = pl.BlockSpec(memory_space=pltpu.VMEM)
DMA = pltpu.SemaphoreType.DMA
LANES = 128
HALF = LANES // 2


def softplus(v):
    return jnp.maximum(v, 0.0) + jnp.log1p(jnp.exp(-jnp.abs(v)))


def bits(n):
    return n.bit_length() - 1


def kernel(
    dims, scale, feat, offer, w_in, w_out, own, live, pos_out, neg_out, loss_out,
    xq, stage, emb, send, recv, pool, near, ids, idc, near_v, near_s, g_src, g_dst, part, ret1, ret2, tall, ysend, yrecv,
    negp, negr, raw, tot, ly, lc, lz,
    bulk_s, bulk_r, y_s, y_r, c_s, c_r, z_s, z_r, local, chunk_sem,
):
    Z, X, C, Y = dims
    XC, N = X * C, Z * X * C
    R = Z * X
    NB, BLK, D = emb.shape
    H = D // C
    CAP = ysend.shape[1]
    RC = Y * CAP
    NEG = pool.shape[3]
    me, q = lax.axis_index("node"), lax.axis_index("rep")
    z, xc = me // XC, me % XC
    x, c = xc // C, xc % C

    def ahead(k):
        dz, dx, dc = k // XC, (k // C) % X, k % C
        return ((z + dz) % Z) * XC + ((x + dx) % X) * C + (c + dc) % C

    def behind(k):
        dz, dx, dc = k // XC, (k // C) % X, k % C
        return ((z + Z - dz) % Z) * XC + ((x + X - dx) % X) * C + (c + C - dc) % C

    def copy(src, dst, s, r, node, rep):
        return pltpu.make_async_remote_copy(
            src_ref=src, dst_ref=dst, send_sem=s, recv_sem=r, device_id=(node, rep), device_id_type=MESH
        )

    def y_stage(n, src, dst):
        return [
            copy(src((q + j) % Y), dst, y_s.at[n, j], y_r.at[n, j], me, (q + j) % Y) for j in range(1, Y)
        ]

    def c_stage(n, src, dst):
        out = []
        for k in range(1, XC):
            to = ahead(k) % XC
            out.append(copy(src(to), dst, c_s.at[n, k], c_r.at[n, k], z * XC + to, q))
        return out

    def z_stage(n, src, dst):
        out = []
        for j in range(1, Z):
            to = (z + j) % Z
            out.append(copy(src(to), dst, z_s.at[n, j], z_r.at[n, j], to * XC + xc, q))
        return out

    def start(copies):
        for each in copies:
            each.start()
        return copies

    def arrived(copies):
        for each in copies:
            each.wait_recv()

    def sent(copies):
        for each in copies:
            each.wait_send()

    def encode(v):
        h = jnp.dot(v, w_in[...], preferred_element_type=jnp.float32)
        h = (0.5 * h * (1.0 + jnp.tanh(0.5 * h))).astype(jnp.bfloat16)
        return jnp.dot(h, w_out[...], preferred_element_type=jnp.float32).astype(jnp.bfloat16)

    barrier = pltpu.get_barrier_semaphore()

    def greet(k, _):
        pl.semaphore_signal(barrier, inc=1, device_id=(ahead(k), q), device_id_type=MESH)
        return 0

    lax.fori_loop(1, N, greet, 0)
    for j in range(1, Y):
        pl.semaphore_signal(barrier, inc=1, device_id=(me, (q + j) % Y), device_id_type=MESH)

    mine = pltpu.make_async_copy(feat.at[:, pl.ds(q * R, R), :], xq, local)
    mine.start()
    slots, per = stage.shape[0], stage.shape[1]
    chunks = NB // per

    def fetch(g, slot):
        return pltpu.make_async_copy(feat.at[pl.ds(g * per, per)], stage.at[slot], chunk_sem.at[slot])

    for g in range(min(slots, chunks)):
        fetch(g, g).start()

    pool[z, x, c] = encode(offer[...]).reshape(NEG, R, D)
    tall[...] = jnp.zeros_like(tall)
    pl.semaphore_wait(barrier, N + Y - 2)
    ids_y = start(y_stage(0, lambda to: own, near.at[q]))
    pool_z = start(z_stage(0, lambda to: pool.at[z, x, c], pool.at[z, x, c]))

    mine.wait()
    G = 16 if NB % 16 == 0 else NB
    n = G * R
    i0 = lax.broadcasted_iota(jnp.int32, (n, n), 0)
    i1 = lax.broadcasted_iota(jnp.int32, (n, n), 1)
    perm = jnp.where(i1 == (i0 & (G - 1)) * R + (i0 >> bits(G)), 1.0, 0.0).astype(jnp.bfloat16)

    def rows(g, _):
        at = pl.multiple_of(g * G, G)
        e = encode(xq[pl.ds(at, G)].reshape(n, D))
        t = jnp.dot(perm, e, preferred_element_type=jnp.float32).astype(jnp.bfloat16)
        for k in range(C):
            send[:, k, pl.ds(at, G), :] = t[:, k * H : (k + 1) * H].reshape(R, G, H)
        return 0

    lax.fori_loop(0, NB // G, rows, 0)

    def bulk(k, to):
        return copy(send.at[to // C, to % C], recv.at[me], bulk_s.at[k], bulk_r.at[k], to, q)

    def bulk_go(k, _):
        bulk(k, ahead(k)).start()
        return 0

    arrived(ids_y)
    mask = own[...]
    for j in range(1, Y):
        mask = mask + near[(q + j) % Y]
    near_v[...] = mask
    ids[z, xc] = mask[0]
    scalars = pltpu.make_async_copy(near_v, near_s, local)
    scalars.start()
    ids_z = start(z_stage(1, lambda to: ids.at[z, xc], ids.at[z, xc]))
    arrived(pool_z)
    pool_x = []
    for dx in range(1, X):
        to = z * XC + ((x + dx) % X) * C + c
        pool_x.append(copy(pool.at[:, x, c], pool.at[:, x, c], c_s.at[0, dx], c_r.at[0, dx], to, q))
    start(pool_x)
    first = N * 3 // 8
    lax.fori_loop(1, first, bulk_go, 0)

    def full(g, _):
        slot = g % slots
        fetch(g, slot).wait()
        emb[pl.ds(g * per, per)] = encode(stage[slot].reshape(per * BLK, D)).reshape(per, BLK, D)

        @pl.when(g + slots < chunks)
        def _():
            fetch(g + slots, slot).start()

        return 0

    lax.fori_loop(0, chunks, full, 0)

    arrived(ids_z)
    ids_c = start(c_stage(2, lambda to: ids.at[:, xc], ids.at[:, xc]))
    arrived(pool_x)
    pool_c = []
    for dc in range(1, C):
        to = z * XC + x * C + (c + dc) % C
        pool_c.append(
            copy(pool.at[:, :, c], pool.at[:, :, c], c_s.at[1, dc], c_r.at[1, dc], to, q)
        )
    start(pool_c)
    lax.fori_loop(first, N, bulk_go, 0)
    recv[me] = send[me // C, me % C]
    scalars.wait()
    arrived(pool_c)

    def negatives(e, _):
        r, o = e >> bits(N), e & (N - 1)
        for k in range(CAP):
            s = near_s[0, r * CAP + k, o]
            p = near_s[1, r * CAP + k, o]
            node = p >> bits(NEG)
            cand = pool[
                node >> bits(XC), (node >> bits(C)) & (X - 1), node & (C - 1), p & (NEG - 1)
            ]
            v = lax.dot_general(
                cand, emb[s], (((1,), (1,)), ((), ())), preferred_element_type=jnp.float32
            )
            negp[r, pl.ds(o * CAP + k, 1), :] = jnp.sum(softplus(v * scale), axis=0, keepdims=True)
        return 0

    lax.fori_loop(0, Y * N, negatives, 0)
    neg_y = start(y_stage(1, lambda to: negp.at[to], negr.at[q]))

    arrived(ids_c)
    lane = lax.broadcasted_iota(jnp.int32, (N, LANES), 1)
    for k in range(RC):
        a = jnp.concatenate(
            [ids[i // XC, i % XC, pl.ds(k, 1), :].astype(jnp.float32) for i in range(N)], axis=0
        )
        t = jnp.swapaxes(jnp.concatenate([a] * (LANES // N), axis=0), 0, 1)[:N]
        idc[pl.ds(k, N, stride=RC), :] = jnp.where(lane < HALF, t, a)

    number = lax.broadcasted_iota(jnp.int32, (N * RC, NB), 1).astype(jnp.float32)

    def pick(ids_col, rows_in):
        hot = jnp.where(ids_col == number, 1.0, 0.0).astype(jnp.bfloat16)
        return jnp.dot(hot, rows_in, preferred_element_type=jnp.float32).astype(jnp.bfloat16)

    def gather(s):
        cols = pltpu.roll(idc[...], (LANES - s) % LANES, 1)
        g_src[s] = pick(cols[:, :1], recv[s])
        g_dst[s] = pick(cols[:, HALF : HALF + 1], recv[s])

    def gather_step(k, _):
        bulk(k, ahead(k)).wait_recv()
        gather(behind(k))
        return 0

    gather(me)
    lax.fori_loop(1, N, gather_step, 0)

    shape = (N, RC, LANES)
    keep = lax.broadcasted_iota(jnp.int32, shape, 0) == lax.broadcasted_iota(jnp.int32, shape, 2)

    def dots(h, _):
        b = g_dst[:, pl.ds(pl.multiple_of(h * 2 * RC, 2 * RC), 2 * RC), :].astype(jnp.float32)
        for k in range(2):
            i = 2 * h + k
            a = g_src[i].astype(jnp.float32).reshape(N, RC, H)
            sums = jnp.sum(a * b[:, k * RC : (k + 1) * RC], axis=2, keepdims=True)
            part[i // XC, i % XC] = jnp.sum(jnp.where(keep, sums, 0.0), axis=0)
        return 0

    lax.fori_loop(0, N // 2, dots, 0)
    back_z = start(z_stage(2, lambda to: part.at[to], ret1.at[z]))
    ret1[z] = part[z]

    arrived(neg_y)
    neg = negp[q]
    for j in range(1, Y):
        neg = neg + negr[(q + j) % Y]
    lit = live[...] > 0.0
    neg = jnp.where(lit, neg * (1.0 / BLK), 0.0)
    neg_out[...] = neg

    arrived(back_z)
    back_c = start(c_stage(3, lambda to: ret1.at[:, to], ret2.at[xc]))
    ret2[xc] = ret1[:, xc]
    arrived(back_c)
    for xx in range(X):
        v = ret2[xx * C]
        for k in range(1, C):
            v = v + ret2[xx * C + k]
        for zz in range(Z):
            at = pl.multiple_of((q * R + zz * X + xx) * RC, RC)
            tall[pl.ds(at, RC), :] = v[zz]
    for r in range(Y):
        for k in range(CAP):
            rows_b = tall[pl.ds(r * CAP + k, BLK, stride=RC), :]
            ysend[r, k] = jnp.swapaxes(rows_b, 0, 1)[:N]
    back_y = start(y_stage(2, lambda to: ysend.at[to], yrecv.at[q]))
    arrived(back_y)
    for k in range(CAP):
        v = ysend[q, k]
        for j in range(1, Y):
            v = v + yrecv[(q + j) % Y, k]
        raw[pl.ds(k, N, stride=CAP), :] = v * scale
    v = raw[...]
    pos_out[...] = jnp.where(lit, v, 0.0)
    loss = jnp.sum(jnp.where(lit, softplus(-v), 0.0) + neg)
    count = jnp.sum(live[...])
    spot = lax.broadcasted_iota(jnp.int32, tot.shape[1:], 1)
    tot[0] = jnp.where(spot == 0, loss, jnp.where(spot == 1, count, 0.0))

    add_y = start(y_stage(3, lambda to: tot.at[0], ly.at[q]))
    arrived(add_y)
    v = tot[0]
    for j in range(1, Y):
        v = v + ly[(q + j) % Y]
    tot[1] = v
    add_c = start(c_stage(4, lambda to: tot.at[1], lc.at[xc]))
    arrived(add_c)
    for k in range(1, XC):
        v = v + lc[behind(k) % XC]
    tot[2] = v
    add_z = start(z_stage(3, lambda to: tot.at[2], lz.at[z]))
    arrived(add_z)
    for j in range(1, Z):
        v = v + lz[(z + j) % Z]
    loss_out[...] = v

    for copies in (ids_y, ids_z, ids_c, pool_z, pool_x, pool_c, neg_y, back_z, back_c, back_y, add_y, add_c, add_z):
        sent(copies)

    def bulk_sent(k, _):
        bulk(k, ahead(k)).wait_send()
        return 0

    lax.fori_loop(1, N, bulk_sent, 0)


def step(dims, features, w_in, w_out, pos_src, pos_dst, counts, neg_blocks, neg_pick):
    Z, X, C, Y = dims
    XC, N, R = X * C, Z * X * C, Z * X
    total, D = features.shape
    BLK = R * Y
    NB = total // BLK
    H = D // C
    CAP = pos_dst.shape[3]
    RC = Y * CAP
    NEG = neg_blocks.shape[1]
    bf, f32, i32 = jnp.bfloat16, jnp.float32, jnp.int32
    scale = 1.0 / D**0.5
    q = lax.axis_index("rep")
    offer = jnp.concatenate(
        [lax.dynamic_slice_in_dim(features, neg_blocks[0, k] * BLK + q * R, R, 0) for k in range(NEG)]
    )

    def slab(a, b):
        pad = ((0, 0), (0, HALF - N))
        t = jnp.concatenate([jnp.pad(a.T, pad), jnp.pad(b.T, pad)], axis=1)
        t = jnp.tile(t, (Y, 1))
        return jnp.where(jnp.arange(RC)[:, None] // CAP == q, t, 0)

    src, dst, pick = (t.reshape(N, CAP) for t in (pos_src, pos_dst, neg_pick))
    own = jnp.stack([slab(src, dst), slab(pick, pick)])
    live = jnp.arange(CAP, dtype=i32)[None, :] < counts.reshape(N, 1)
    live = jnp.broadcast_to(live.astype(f32).reshape(N * CAP, 1), (N * CAP, BLK))
    per, slots = (8, 4) if NB % 8 == 0 else (NB, 1)
    scratch = [
        pltpu.VMEM((NB, R, D), bf),
        pltpu.VMEM((slots, per, BLK, D), bf),
        pltpu.VMEM((NB, BLK, D), bf),
        pltpu.VMEM((R, C, NB, H), bf),
        pltpu.VMEM((N, NB, H), bf),
        pltpu.VMEM((Z, X, C, NEG, R, D), bf),
        pltpu.VMEM((Y, 2, RC, LANES), i32),
        pltpu.VMEM((Z, XC, RC, LANES), i32),
        pltpu.VMEM((N * RC, LANES), f32),
        pltpu.VMEM((2, RC, LANES), i32),
        pltpu.SMEM((2, RC, LANES), i32),
        pltpu.VMEM((N, N * RC, H), bf),
        pltpu.VMEM((N, N * RC, H), bf),
        pltpu.VMEM((Z, XC, RC, LANES), f32),
        pltpu.VMEM((Z, XC, RC, LANES), f32),
        pltpu.VMEM((XC, Z, RC, LANES), f32),
        pltpu.VMEM((BLK * RC, LANES), f32),
        pltpu.VMEM((Y, CAP, N, BLK), f32),
        pltpu.VMEM((Y, CAP, N, BLK), f32),
        pltpu.VMEM((Y, N * CAP, BLK), f32),
        pltpu.VMEM((Y, N * CAP, BLK), f32),
        pltpu.VMEM((N * CAP, BLK), f32),
        pltpu.VMEM((3, 8, LANES), f32),
        pltpu.VMEM((Y, 8, LANES), f32),
        pltpu.VMEM((XC, 8, LANES), f32),
        pltpu.VMEM((Z, 8, LANES), f32),
        DMA((N,)),
        DMA((N,)),
        DMA((4, Y)),
        DMA((4, Y)),
        DMA((5, XC)),
        DMA((5, XC)),
        DMA((4, Z)),
        DMA((4, Z)),
        DMA,
        DMA((slots,)),
    ]
    pos, neg, sums = pl.pallas_call(
        functools.partial(kernel, dims, scale),
        in_specs=[pl.BlockSpec(memory_space=pl.ANY)] + [VMEM] * 5,
        out_specs=[VMEM] * 3,
        out_shape=[
            jax.ShapeDtypeStruct((N * CAP, BLK), f32),
            jax.ShapeDtypeStruct((N * CAP, BLK), f32),
            jax.ShapeDtypeStruct((8, LANES), f32),
        ],
        scratch_shapes=scratch,
        compiler_params=pltpu.CompilerParams(
            collective_id=0, has_side_effects=True, vmem_limit_bytes=60 * 2**20
        ),
        name="step",
    )(features.reshape(NB, BLK, D), offer, w_in, w_out, own, live)
    loss = sums[0, 0] / sums[0, 1]
    shape = (1, 1, N, CAP, BLK)
    return pos.reshape(shape), neg.reshape(shape), loss


def solution(mesh):
    n, reps = mesh.shape["node"], mesh.shape["rep"]
    dims = (n // 8, 4, 2, reps) if n >= 32 else (n // 4, 2, 2, reps)
    return jax.shard_map(
        functools.partial(step, dims),
        mesh=mesh,
        in_specs=(
            P("node", None),
            P(),
            P(),
            P("node", "rep", None, None),
            P("node", "rep", None, None),
            P("node", "rep", None),
            P("node", None),
            P("node", "rep", None, None),
        ),
        out_specs=(P("node", "rep", None, None, None), P("node", "rep", None, None, None), P()),
        check_vma=False,
    )
```

time: 339 us -> 182 us (0.54)
  Pallas kernels: 0 us -> 166 us
  waiting for transfers between devices: 161 us -> 0 us
  blocking collectives: 65.1 us -> 0 us
  local copies, waits for them, and re-layouts: 37.1 us -> 7.2 us
  other arithmetic: 30 us -> 3.62 us
  matrix products: 20.8 us -> 0 us
  between operations: 18.6 us -> 4.46 us
  starting transfers between devices: 5.93 us -> 0 us
    pallas_call x0 -> x1, Pallas kernels: none -> 166 us  [step(): pl.pallas_call(functools.partial(kernel, dims, scale), in_specs=[pl.Block...]
    all_to_all x1 -> x0, waiting for transfers between devices: 88.5 us -> none  [shards(): lax.all_to_all(reply, NODE, split_axis=0, concat_axis=0, tiled=True)]
    all_gather x1 -> x0, waiting for transfers between devices: 72.6 us -> none  [shards(): pool = lax.all_gather(offered, NODE, axis=0, tiled=True)]
    psum x4 -> x0, blocking collectives: 42.9 us -> none  [by_axis(): value = lax.psum(value, axis)]
    gather x4 -> x0, local copies, waits for them, and re-layouts: 35.8 us -> none  [the longest x1 10.7 us: shards(): jnp.take(blocks, lax.all_to_all(asked_ids, NODE, split_axis=0, concat_axi...]
    all_to_all x1 -> x0, blocking collectives: 22.2 us -> none  [shards(): lax.all_to_all(asked_ids, NODE, split_axis=0, concat_axis=0, tiled=True)]
    dot_general x2 -> x0, matrix products: 20.8 us -> none  [the longest x1 10.9 us: encode(): jnp.dot(hidden, w_out, preferred_element_type=jnp.float32)]
    reduce_sum x3 -> x0, other arithmetic: 10.6 us -> none  [the longest x1 8.53 us: shards(): neg_out = jnp.where(livex, jnp.mean(jax.nn.softplus(scores), axis=-1), 0.0)]
  transfers between devices with their start and end apart: 2 -> 0, of which waited for: 2 -> 0; matrix products, arithmetic and copies ran while one was open for 18% -> 0% of each run, Pallas kernels for 0% -> 0%
where the time goes in v2:
time: 182 us
  Pallas kernels  166 us (91%)
  local copies, waits for them, and re-layouts  7.2 us (4%)
  between operations  4.46 us (2%)
  other arithmetic  3.62 us (2%)
    pallas_call x1, Pallas kernels, step(): pl.pallas_call(functools.partial(kernel, dims, scale), in_specs=[pl.Block...  166 us

profile of v2, /device:TPU:1, one launch (start us, length us, event | category | flops | bytes accessed | tf_op | source)
XLA Modules:
  0.0 181.5 jit_solution(16696366538383933426)
XLA Ops:
  0.6 0.8 pad_add_fusion.1
  1.4 0.8 pad_add_fusion.2
  2.2 1.3 fusion.3
  4.9 0.1 bitcast_select_fusion.1
  5.0 0.6 pad_add_fusion.own
  5.6 0.7 constant_dynamic-slice_fusion.1
  6.3 0.6 pad_maximum_fusion.offer
  6.9 0.7 fusion
  7.7 0.1 reshape.164
  7.8 0.7 broadcast_in_dim.26.live
  8.5 166.3 %step.1 = (f32[128,128]{1,0:T(8,128)}, f32[128,128]{1,0:T(8,128)}, f32[8,128]{1,0:T(8,128)}) custom-call(bf16[160,128,256]{2,1,0:T(8,128)(2,1)} %bitcast.21, bf16[64,256]{1,0:T(8,128)(2,1)} %pad_maximum_fusion.offer, bf16[256,256]{1,0:T(8,128)(2,1)} %w_in.1, bf16[256,256]{1,0:T(8,128)(2,1)} %w_out.1, s32[2,8,128]{2,1,0:T(8,128)} %pad_add_fusion.own, ...), custom_call_target="tpu_custom_call" | custom-call | tf_op jit(solution)/shard_map/step/pallas_call | solution.py:382
  174.8 1.3 fusion.2
  177.5 1.5 copy.13
  178.9 1.5 copy.14
  (3 shorter events, 0.0 us)

commit v3 on v2

--- a/solution.py
+++ b/solution.py
@@ -23,10 +23,10 @@
 
 
 def kernel(
-    dims, scale, feat, offer, w_in, w_out, own, live, pos_out, neg_out, loss_out,
-    xq, stage, emb, send, recv, pool, near, ids, idc, near_v, near_s, g_src, g_dst, part, ret1, ret2, tall, ysend, yrecv,
-    negp, negr, raw, tot, ly, lc, lz,
-    bulk_s, bulk_r, y_s, y_r, c_s, c_r, z_s, z_r, local, chunk_sem,
+    dims, scale, feat, chosen, w_in, w_out, own, pos_out, neg_out, loss_out,
+    xq, stage, emb, send, recv, pool, near, ids, idc, near_v, near_s, ends, part, other, half, ret, tall, ysend, yrecv,
+    negp, negr, tot, lp, ly,
+    bulk_s, bulk_r, back_s, back_r, loss_s, loss_r, y_s, y_r, c_s, c_r, z_s, z_r, die, local, chunk_sem,
 ):
     Z, X, C, Y = dims
     XC, N = X * C, Z * X * C
@@ -111,13 +111,16 @@
     for g in range(min(slots, chunks)):
         fetch(g, g).start()
 
-    pool[z, x, c] = encode(offer[...]).reshape(NEG, R, D)
     tall[...] = jnp.zeros_like(tall)
+    fill = lax.broadcasted_iota(jnp.int32, (2, RC, LANES), 1) // CAP == q
+    near_v[...] = jnp.where(fill, jnp.concatenate([own[...]] * Y, axis=1), 0)
+    mine.wait()
+    offer = jnp.concatenate([xq[chosen[0, k]] for k in range(NEG)], axis=0)
+    pool[z, x, c] = encode(offer).reshape(NEG, R, D)
     pl.semaphore_wait(barrier, N + Y - 2)
-    ids_y = start(y_stage(0, lambda to: own, near.at[q]))
+    ids_y = start(y_stage(0, lambda to: near_v, near.at[q]))
     pool_z = start(z_stage(0, lambda to: pool.at[z, x, c], pool.at[z, x, c]))
 
-    mine.wait()
     G = 16 if NB % 16 == 0 else NB
     n = G * R
     i0 = lax.broadcasted_iota(jnp.int32, (n, n), 0)
@@ -134,29 +137,30 @@
 
     lax.fori_loop(0, NB // G, rows, 0)
 
-    def bulk(k, to):
+    def bulk(k):
+        to = ahead(k)
         return copy(send.at[to // C, to % C], recv.at[me], bulk_s.at[k], bulk_r.at[k], to, q)
 
     def bulk_go(k, _):
-        bulk(k, ahead(k)).start()
+        bulk(k).start()
         return 0
 
     arrived(ids_y)
-    mask = own[...]
+    tile = near_v[...]
     for j in range(1, Y):
-        mask = mask + near[(q + j) % Y]
-    near_v[...] = mask
-    ids[z, xc] = mask[0]
-    scalars = pltpu.make_async_copy(near_v, near_s, local)
+        tile = tile + near[(q + j) % Y]
+    near[q] = tile
+    ids[z, xc] = tile[0]
+    ids_z = start(z_stage(1, lambda to: ids.at[z, xc], ids.at[z, xc]))
+    scalars = pltpu.make_async_copy(near.at[q], near_s, local)
     scalars.start()
-    ids_z = start(z_stage(1, lambda to: ids.at[z, xc], ids.at[z, xc]))
     arrived(pool_z)
     pool_x = []
     for dx in range(1, X):
         to = z * XC + ((x + dx) % X) * C + c
         pool_x.append(copy(pool.at[:, x, c], pool.at[:, x, c], c_s.at[0, dx], c_r.at[0, dx], to, q))
     start(pool_x)
-    first = N * 3 // 8
+    first = N // 4
     lax.fori_loop(1, first, bulk_go, 0)
 
     def full(g, _):
@@ -188,21 +192,25 @@
     arrived(pool_c)
 
     def negatives(e, _):
-        r, o = e >> bits(N), e & (N - 1)
-        for k in range(CAP):
-            s = near_s[0, r * CAP + k, o]
-            p = near_s[1, r * CAP + k, o]
+        for k in range(2 * CAP):
+            r, o = e >> bits(N // 2), (e & (N // 2 - 1)) * 2 + k // CAP
+            s = near_s[0, r * CAP + k % CAP, o]
+            p = near_s[1, r * CAP + k % CAP, o]
             node = p >> bits(NEG)
             cand = pool[
                 node >> bits(XC), (node >> bits(C)) & (X - 1), node & (C - 1), p & (NEG - 1)
             ]
             v = lax.dot_general(
-                cand, emb[s], (((1,), (1,)), ((), ())), preferred_element_type=jnp.float32
+                cand,
+                emb[jnp.maximum(s, 0)],
+                (((1,), (1,)), ((), ())),
+                preferred_element_type=jnp.float32,
             )
-            negp[r, pl.ds(o * CAP + k, 1), :] = jnp.sum(softplus(v * scale), axis=0, keepdims=True)
-        return 0
-
-    lax.fori_loop(0, Y * N, negatives, 0)
+            total = jnp.sum(softplus(v * scale), axis=0, keepdims=True)
+            negp[r, pl.ds(o * CAP + k % CAP, 1), :] = jnp.where(s >= 0, total, 0.0)
+        return 0
+
+    lax.fori_loop(0, Y * N // 2, negatives, 0)
     neg_y = start(y_stage(1, lambda to: negp.at[to], negr.at[q]))
 
     arrived(ids_c)
@@ -214,19 +222,17 @@
         t = jnp.swapaxes(jnp.concatenate([a] * (LANES // N), axis=0), 0, 1)[:N]
         idc[pl.ds(k, N, stride=RC), :] = jnp.where(lane < HALF, t, a)
 
-    number = lax.broadcasted_iota(jnp.int32, (N * RC, NB), 1).astype(jnp.float32)
-
-    def pick(ids_col, rows_in):
-        hot = jnp.where(ids_col == number, 1.0, 0.0).astype(jnp.bfloat16)
-        return jnp.dot(hot, rows_in, preferred_element_type=jnp.float32).astype(jnp.bfloat16)
+    number = lax.broadcasted_iota(jnp.int32, (2 * N * RC, NB), 1).astype(jnp.float32)
 
     def gather(s):
         cols = pltpu.roll(idc[...], (LANES - s) % LANES, 1)
-        g_src[s] = pick(cols[:, :1], recv[s])
-        g_dst[s] = pick(cols[:, HALF : HALF + 1], recv[s])
+        col = jnp.concatenate([cols[:, :1], cols[:, HALF : HALF + 1]], axis=0)
+        hot = jnp.where(col == number, 1.0, 0.0).astype(jnp.bfloat16)
+        got = jnp.dot(hot, recv[s], preferred_element_type=jnp.float32).astype(jnp.bfloat16)
+        ends[s] = got.reshape(2, N * RC, H)
 
     def gather_step(k, _):
-        bulk(k, ahead(k)).wait_recv()
+        bulk(k).wait_recv()
         gather(behind(k))
         return 0
 
@@ -237,80 +243,104 @@
     keep = lax.broadcasted_iota(jnp.int32, shape, 0) == lax.broadcasted_iota(jnp.int32, shape, 2)
 
     def dots(h, _):
-        b = g_dst[:, pl.ds(pl.multiple_of(h * 2 * RC, 2 * RC), 2 * RC), :].astype(jnp.float32)
+        at = pl.multiple_of(h * 2 * RC, 2 * RC)
+        b = ends[:, 1, pl.ds(at, 2 * RC), :].astype(jnp.float32)
         for k in range(2):
             i = 2 * h + k
-            a = g_src[i].astype(jnp.float32).reshape(N, RC, H)
+            a = ends[i, 0].astype(jnp.float32).reshape(N, RC, H)
             sums = jnp.sum(a * b[:, k * RC : (k + 1) * RC], axis=2, keepdims=True)
-            part[i // XC, i % XC] = jnp.sum(jnp.where(keep, sums, 0.0), axis=0)
+            part[i // XC, (i % XC) // C, i % C] = jnp.sum(jnp.where(keep, sums, 0.0), axis=0)
         return 0
 
     lax.fori_loop(0, N // 2, dots, 0)
-    back_z = start(z_stage(2, lambda to: part.at[to], ret1.at[z]))
-    ret1[z] = part[z]
-
+
+    to = z * XC + x * C + (c + 1) % C
+    swap = copy(part.at[:, :, (c + 1) % C], other, die.at[0], die.at[1], to, q)
+    swap.start()
     arrived(neg_y)
     neg = negp[q]
     for j in range(1, Y):
         neg = neg + negr[(q + j) % Y]
-    lit = live[...] > 0.0
-    neg = jnp.where(lit, neg * (1.0 / BLK), 0.0)
+    neg = neg * (1.0 / BLK)
     neg_out[...] = neg
-
-    arrived(back_z)
-    back_c = start(c_stage(3, lambda to: ret1.at[:, to], ret2.at[xc]))
-    ret2[xc] = ret1[:, xc]
-    arrived(back_c)
-    for xx in range(X):
-        v = ret2[xx * C]
-        for k in range(1, C):
-            v = v + ret2[xx * C + k]
-        for zz in range(Z):
-            at = pl.multiple_of((q * R + zz * X + xx) * RC, RC)
-            tall[pl.ds(at, RC), :] = v[zz]
+    loss = jnp.sum(neg)
+    edge = lax.broadcasted_iota(jnp.int32, (CAP, LANES), 1) < N
+    count = jnp.sum(jnp.where(edge & (own[0] >= 0), 1.0, 0.0)) * BLK
+    swap.wait_recv()
+    v = (part[:, :, c] + other[...]) * scale
+    half[...] = v
+
+    def back(k):
+        to = ((z + k // X) % Z) * XC + ((x + k % X) % X) * C + c
+        return copy(half.at[to // XC, (to % XC) // C], ret.at[z, x], back_s.at[k], back_r.at[k], to, q)
+
+    def back_go(k, _):
+        back(k).start()
+        return 0
+
+    def back_got(k, _):
+        back(k).wait_recv()
+        return 0
+
+    lax.fori_loop(1, R, back_go, 0)
+    lit = jnp.concatenate([ids[:, k * C + c][:, None] for k in range(X)], axis=1) >= 0
+    lit = lit & (lax.broadcasted_iota(jnp.int32, (Z, X, RC, LANES), 3) < N)
+    loss = loss + jnp.sum(jnp.where(lit, softplus(-v), 0.0))
+    spot = lax.broadcasted_iota(jnp.int32, tot.shape[1:], 1)
+    mine_sum = jnp.where(spot == 0, loss, jnp.where(spot == 1, count, 0.0))
+    tot[0] = mine_sum
+    ret[z, x] = half[z, x]
+
+    def add(k):
+        return copy(tot.at[0], lp.at[me], loss_s.at[k], loss_r.at[k], ahead(k), q)
+
+    def add_go(k, _):
+        add(k).start()
+        return 0
+
+    def add_got(k, v):
+        add(k).wait_recv()
+        return v + lp[behind(k)]
+
+    lax.fori_loop(1, N, add_go, 0)
+    lax.fori_loop(1, R, back_got, 0)
+    for k in range(R):
+        at = pl.multiple_of((q * R + k) * RC, RC)
+        tall[pl.ds(at, RC), :] = ret[k // X, k % X]
     for r in range(Y):
         for k in range(CAP):
             rows_b = tall[pl.ds(r * CAP + k, BLK, stride=RC), :]
             ysend[r, k] = jnp.swapaxes(rows_b, 0, 1)[:N]
     back_y = start(y_stage(2, lambda to: ysend.at[to], yrecv.at[q]))
+    total = lax.fori_loop(1, N, add_got, mine_sum)
+    tot[1] = total
+    add_y = start(y_stage(3, lambda to: tot.at[1], ly.at[q]))
     arrived(back_y)
     for k in range(CAP):
         v = ysend[q, k]
         for j in range(1, Y):
             v = v + yrecv[(q + j) % Y, k]
-        raw[pl.ds(k, N, stride=CAP), :] = v * scale
-    v = raw[...]
-    pos_out[...] = jnp.where(lit, v, 0.0)
-    loss = jnp.sum(jnp.where(lit, softplus(-v), 0.0) + neg)
-    count = jnp.sum(live[...])
-    spot = lax.broadcasted_iota(jnp.int32, tot.shape[1:], 1)
-    tot[0] = jnp.where(spot == 0, loss, jnp.where(spot == 1, count, 0.0))
-
-    add_y = start(y_stage(3, lambda to: tot.at[0], ly.at[q]))
+        pos_out[pl.ds(k, N, stride=CAP), :] = v
     arrived(add_y)
-    v = tot[0]
     for j in range(1, Y):
-        v = v + ly[(q + j) % Y]
-    tot[1] = v
-    add_c = start(c_stage(4, lambda to: tot.at[1], lc.at[xc]))
-    arrived(add_c)
-    for k in range(1, XC):
-        v = v + lc[behind(k) % XC]
-    tot[2] = v
-    add_z = start(z_stage(3, lambda to: tot.at[2], lz.at[z]))
-    arrived(add_z)
-    for j in range(1, Z):
-        v = v + lz[(z + j) % Z]
-    loss_out[...] = v
-
-    for copies in (ids_y, ids_z, ids_c, pool_z, pool_x, pool_c, neg_y, back_z, back_c, back_y, add_y, add_c, add_z):
+        total = total + ly[(q + j) % Y]
+    loss_out[...] = total
+
+    for copies in (ids_y, ids_z, ids_c, pool_z, pool_x, pool_c, neg_y, back_y, add_y):
         sent(copies)
+    swap.wait_send()
 
     def bulk_sent(k, _):
-        bulk(k, ahead(k)).wait_send()
+        bulk(k).wait_send()
+        add(k).wait_send()
+        return 0
+
+    def back_sent(k, _):
+        back(k).wait_send()
         return 0
 
     lax.fori_loop(1, N, bulk_sent, 0)
+    lax.fori_loop(1, R, back_sent, 0)
 
 
 def step(dims, features, w_in, w_out, pos_src, pos_dst, counts, neg_blocks, neg_pick):
@@ -325,21 +355,11 @@
     NEG = neg_blocks.shape[1]
     bf, f32, i32 = jnp.bfloat16, jnp.float32, jnp.int32
     scale = 1.0 / D**0.5
-    q = lax.axis_index("rep")
-    offer = jnp.concatenate(
-        [lax.dynamic_slice_in_dim(features, neg_blocks[0, k] * BLK + q * R, R, 0) for k in range(NEG)]
-    )
-
-    def slab(a, b):
-        pad = ((0, 0), (0, HALF - N))
-        t = jnp.concatenate([jnp.pad(a.T, pad), jnp.pad(b.T, pad)], axis=1)
-        t = jnp.tile(t, (Y, 1))
-        return jnp.where(jnp.arange(RC)[:, None] // CAP == q, t, 0)
-
     src, dst, pick = (t.reshape(N, CAP) for t in (pos_src, pos_dst, neg_pick))
-    own = jnp.stack([slab(src, dst), slab(pick, pick)])
     live = jnp.arange(CAP, dtype=i32)[None, :] < counts.reshape(N, 1)
-    live = jnp.broadcast_to(live.astype(f32).reshape(N * CAP, 1), (N * CAP, BLK))
+    own = jnp.stack([jnp.where(live, src, -1), dst, pick, pick])
+    own = jnp.transpose(own.reshape(2, 2, N, CAP), (0, 3, 1, 2))
+    own = jnp.pad(own, ((0, 0), (0, 0), (0, 0), (0, HALF - N))).reshape(2, CAP, LANES)
     per, slots = (8, 4) if NB % 8 == 0 else (NB, 1)
     scratch = [
         pltpu.VMEM((NB, R, D), bf),
@@ -353,35 +373,38 @@
         pltpu.VMEM((N * RC, LANES), f32),
         pltpu.VMEM((2, RC, LANES), i32),
         pltpu.SMEM((2, RC, LANES), i32),
-        pltpu.VMEM((N, N * RC, H), bf),
-        pltpu.VMEM((N, N * RC, H), bf),
-        pltpu.VMEM((Z, XC, RC, LANES), f32),
-        pltpu.VMEM((Z, XC, RC, LANES), f32),
-        pltpu.VMEM((XC, Z, RC, LANES), f32),
+        pltpu.VMEM((N, 2, N * RC, H), bf),
+        pltpu.VMEM((Z, X, C, RC, LANES), f32),
+        pltpu.VMEM((Z, X, RC, LANES), f32),
+        pltpu.VMEM((Z, X, RC, LANES), f32),
+        pltpu.VMEM((Z, X, RC, LANES), f32),
         pltpu.VMEM((BLK * RC, LANES), f32),
         pltpu.VMEM((Y, CAP, N, BLK), f32),
         pltpu.VMEM((Y, CAP, N, BLK), f32),
         pltpu.VMEM((Y, N * CAP, BLK), f32),
         pltpu.VMEM((Y, N * CAP, BLK), f32),
-        pltpu.VMEM((N * CAP, BLK), f32),
-        pltpu.VMEM((3, 8, LANES), f32),
+        pltpu.VMEM((2, 8, LANES), f32),
+        pltpu.VMEM((N, 8, LANES), f32),
         pltpu.VMEM((Y, 8, LANES), f32),
-        pltpu.VMEM((XC, 8, LANES), f32),
-        pltpu.VMEM((Z, 8, LANES), f32),
+        DMA((N,)),
+        DMA((N,)),
+        DMA((R,)),
+        DMA((R,)),
         DMA((N,)),
         DMA((N,)),
         DMA((4, Y)),
         DMA((4, Y)),
-        DMA((5, XC)),
-        DMA((5, XC)),
-        DMA((4, Z)),
-        DMA((4, Z)),
+        DMA((3, XC)),
+        DMA((3, XC)),
+        DMA((2, Z)),
+        DMA((2, Z)),
+        DMA((2,)),
         DMA,
         DMA((slots,)),
     ]
     pos, neg, sums = pl.pallas_call(
         functools.partial(kernel, dims, scale),
-        in_specs=[pl.BlockSpec(memory_space=pl.ANY)] + [VMEM] * 5,
+        in_specs=[pl.BlockSpec(memory_space=pl.ANY), pl.BlockSpec(memory_space=pltpu.SMEM)] + [VMEM] * 3,
         out_specs=[VMEM] * 3,
         out_shape=[
             jax.ShapeDtypeStruct((N * CAP, BLK), f32),
@@ -393,7 +416,7 @@
             collective_id=0, has_side_effects=True, vmem_limit_bytes=60 * 2**20
         ),
         name="step",
-    )(features.reshape(NB, BLK, D), offer, w_in, w_out, own, live)
+    )(features.reshape(NB, BLK, D), neg_blocks, w_in, w_out, own)
     loss = sums[0, 0] / sums[0, 1]
     shape = (1, 1, N, CAP, BLK)
     return pos.reshape(shape), neg.reshape(shape), loss

time: 182 us -> 146 us (0.80)
  Pallas kernels: 166 us -> 137 us
  local copies, waits for them, and re-layouts: 7.2 us -> 4.94 us
  other arithmetic: 3.62 us -> 1.45 us
    pallas_call x1, Pallas kernels: 166 us -> 137 us  [step(): pl.pallas_call(functools.partial(kernel, dims, scale), in_specs=[pl.Block...]
    concatenate x3 -> x0, other arithmetic: 2.22 us -> none  [the longest x2 1.6 us: slab(): t = jnp.concatenate([jnp.pad(a.T, pad), jnp.pad(b.T, pad)], axis=1)]
where the time goes in v3:
time: 146 us
  Pallas kernels  137 us (94%)
  local copies, waits for them, and re-layouts  4.94 us (3%)
  between operations  3.11 us (2%)
    pallas_call x1, Pallas kernels, step(): pl.pallas_call(functools.partial(kernel, dims, scale), in_specs=[pl.Block...  137 us
    unnamed x2, local copies, waits for them, and re-layouts  2.95 us

profile of v3, /device:TPU:1, one launch (start us, length us, event | category | flops | bytes accessed | tf_op | source)
XLA Modules:
  0.0 146.0 jit_solution(9898209883122603672)
XLA Ops:
  0.6 0.7 compare_select_fusion
  1.3 0.8 pad_add_fusion
  2.1 0.7 reshape.78.own
  2.7 136.5 %step.1 = (f32[128,128]{1,0:T(8,128)}, f32[128,128]{1,0:T(8,128)}, f32[8,128]{1,0:T(8,128)}) custom-call(bf16[160,128,256]{2,1,0:T(8,128)(2,1)} %bitcast.13, s32[1,2]{1,0:T(1,128)} %chosen.1, bf16[256,256]{1,0:T(8,128)(2,1)} %w_in.1, bf16[256,256]{1,0:T(8,128)(2,1)} %w_out.1, s32[2,2,128]{2,1,0:T(2,128)} %reshape.78.own), custom_call_target="tpu_custom_call" | custom-call | tf_op jit(solution)/shard_map/step/pallas_call | solution.py:405
  139.3 1.3 fusion
  142.0 1.5 %copy.16 = f32[1,1,64,2,128]{4,3,2,1,0:T(2,128)} copy(f32[1,1,64,2,128]{4,3,2,1,0:T(2,128)} %bitcast.15) | data formatting | bytes 131072
  143.4 1.5 %copy.17 = f32[1,1,64,2,128]{4,3,2,1,0:T(2,128)} copy(f32[1,1,64,2,128]{4,3,2,1,0:T(2,128)} %bitcast.14) | data formatting | bytes 131072
  (1 shorter events, 0.0 us)

commit v4 on v3

--- a/solution.py
+++ b/solution.py
@@ -25,8 +25,8 @@
 def kernel(
     dims, scale, feat, chosen, w_in, w_out, own, pos_out, neg_out, loss_out,
     xq, stage, emb, send, recv, pool, near, ids, idc, near_v, near_s, ends, part, other, half, ret, tall, ysend, yrecv,
-    negp, negr, tot, lp, ly,
-    bulk_s, bulk_r, back_s, back_r, loss_s, loss_r, y_s, y_r, c_s, c_r, z_s, z_r, die, local, chunk_sem,
+    negp, negr, tot, lc, lz, ly,
+    bulk_s, bulk_r, back_s, back_r, y_s, y_r, c_s, c_r, z_s, z_r, die, local, chunk_sem,
 ):
     Z, X, C, Y = dims
     XC, N = X * C, Z * X * C
@@ -96,7 +96,10 @@
         pl.semaphore_signal(barrier, inc=1, device_id=(ahead(k), q), device_id_type=MESH)
         return 0
 
-    lax.fori_loop(1, N, greet, 0)
+    lax.fori_loop(1, XC, greet, 0)
+    for j in range(1, Z):
+        to = ((z + j) % Z) * XC + xc
+        pl.semaphore_signal(barrier, inc=1, device_id=(to, q), device_id_type=MESH)
     for j in range(1, Y):
         pl.semaphore_signal(barrier, inc=1, device_id=(me, (q + j) % Y), device_id_type=MESH)
 
@@ -117,7 +120,7 @@
     mine.wait()
     offer = jnp.concatenate([xq[chosen[0, k]] for k in range(NEG)], axis=0)
     pool[z, x, c] = encode(offer).reshape(NEG, R, D)
-    pl.semaphore_wait(barrier, N + Y - 2)
+    pl.semaphore_wait(barrier, XC + Z + Y - 3)
     ids_y = start(y_stage(0, lambda to: near_v, near.at[q]))
     pool_z = start(z_stage(0, lambda to: pool.at[z, x, c], pool.at[z, x, c]))
 
@@ -141,8 +144,20 @@
         to = ahead(k)
         return copy(send.at[to // C, to % C], recv.at[me], bulk_s.at[k], bulk_r.at[k], to, q)
 
-    def bulk_go(k, _):
-        bulk(k).start()
+    def column(m):
+        return bulk((m // C) * XC + m % C)
+
+    side = (X - 1) * C
+
+    def others(m):
+        return bulk((m // side) * XC + C + m % side)
+
+    def column_go(m, _):
+        column(m).start()
+        return 0
+
+    def others_go(m, _):
+        others(m).start()
         return 0
 
     arrived(ids_y)
@@ -160,8 +175,8 @@
         to = z * XC + ((x + dx) % X) * C + c
         pool_x.append(copy(pool.at[:, x, c], pool.at[:, x, c], c_s.at[0, dx], c_r.at[0, dx], to, q))
     start(pool_x)
-    first = N // 4
-    lax.fori_loop(1, first, bulk_go, 0)
+    lax.fori_loop(1, Z * C, column_go, 0)
+    recv[me] = send[me // C, me % C]
 
     def full(g, _):
         slot = g % slots
@@ -174,10 +189,10 @@
 
         return 0
 
-    lax.fori_loop(0, chunks, full, 0)
-
+    lax.fori_loop(0, chunks // 4, full, 0)
     arrived(ids_z)
     ids_c = start(c_stage(2, lambda to: ids.at[:, xc], ids.at[:, xc]))
+    lax.fori_loop(chunks // 4, chunks, full, 0)
     arrived(pool_x)
     pool_c = []
     for dc in range(1, C):
@@ -186,8 +201,7 @@
             copy(pool.at[:, :, c], pool.at[:, :, c], c_s.at[1, dc], c_r.at[1, dc], to, q)
         )
     start(pool_c)
-    lax.fori_loop(first, N, bulk_go, 0)
-    recv[me] = send[me // C, me % C]
+    lax.fori_loop(0, Z * side, others_go, 0)
     scalars.wait()
     arrived(pool_c)
 
@@ -231,13 +245,19 @@
         got = jnp.dot(hot, recv[s], preferred_element_type=jnp.float32).astype(jnp.bfloat16)
         ends[s] = got.reshape(2, N * RC, H)
 
-    def gather_step(k, _):
-        bulk(k).wait_recv()
-        gather(behind(k))
+    def gather_column(m, _):
+        column(m).wait_recv()
+        gather(behind((m // C) * XC + m % C))
+        return 0
+
+    def gather_others(m, _):
+        others(m).wait_recv()
+        gather(behind((m // side) * XC + C + m % side))
         return 0
 
     gather(me)
-    lax.fori_loop(1, N, gather_step, 0)
+    lax.fori_loop(1, Z * C, gather_column, 0)
+    lax.fori_loop(0, Z * side, gather_others, 0)
 
     shape = (N, RC, LANES)
     keep = lax.broadcasted_iota(jnp.int32, shape, 0) == lax.broadcasted_iota(jnp.int32, shape, 2)
@@ -261,14 +281,14 @@
     neg = negp[q]
     for j in range(1, Y):
         neg = neg + negr[(q + j) % Y]
-    neg = neg * (1.0 / BLK)
     neg_out[...] = neg
-    loss = jnp.sum(neg)
+    loss = jnp.sum(neg) * (1.0 / BLK)
     edge = lax.broadcasted_iota(jnp.int32, (CAP, LANES), 1) < N
     count = jnp.sum(jnp.where(edge & (own[0] >= 0), 1.0, 0.0)) * BLK
     swap.wait_recv()
-    v = (part[:, :, c] + other[...]) * scale
+    v = part[:, :, c] + other[...]
     half[...] = v
+    v = v * scale
 
     def back(k):
         to = ((z + k // X) % Z) * XC + ((x + k % X) % X) * C + c
@@ -291,19 +311,14 @@
     tot[0] = mine_sum
     ret[z, x] = half[z, x]
 
-    def add(k):
-        return copy(tot.at[0], lp.at[me], loss_s.at[k], loss_r.at[k], ahead(k), q)
-
-    def add_go(k, _):
-        add(k).start()
-        return 0
-
-    def add_got(k, v):
-        add(k).wait_recv()
-        return v + lp[behind(k)]
-
-    lax.fori_loop(1, N, add_go, 0)
+    add_c = start(c_stage(3, lambda to: tot.at[0], lc.at[xc]))
     lax.fori_loop(1, R, back_got, 0)
+    arrived(add_c)
+    total = mine_sum
+    for k in range(1, XC):
+        total = total + lc[behind(k) % XC]
+    tot[1] = total
+    add_z = start(z_stage(2, lambda to: tot.at[1], lz.at[z]))
     for k in range(R):
         at = pl.multiple_of((q * R + k) * RC, RC)
         tall[pl.ds(at, RC), :] = ret[k // X, k % X]
@@ -312,9 +327,11 @@
             rows_b = tall[pl.ds(r * CAP + k, BLK, stride=RC), :]
             ysend[r, k] = jnp.swapaxes(rows_b, 0, 1)[:N]
     back_y = start(y_stage(2, lambda to: ysend.at[to], yrecv.at[q]))
-    total = lax.fori_loop(1, N, add_got, mine_sum)
-    tot[1] = total
-    add_y = start(y_stage(3, lambda to: tot.at[1], ly.at[q]))
+    arrived(add_z)
+    for j in range(1, Z):
+        total = total + lz[(z + j) % Z]
+    tot[2] = total
+    add_y = start(y_stage(3, lambda to: tot.at[2], ly.at[q]))
     arrived(back_y)
     for k in range(CAP):
         v = ysend[q, k]
@@ -326,13 +343,12 @@
         total = total + ly[(q + j) % Y]
     loss_out[...] = total
 
-    for copies in (ids_y, ids_z, ids_c, pool_z, pool_x, pool_c, neg_y, back_y, add_y):
+    for copies in (ids_y, ids_z, ids_c, pool_z, pool_x, pool_c, neg_y, back_y, add_c, add_z, add_y):
         sent(copies)
     swap.wait_send()
 
     def bulk_sent(k, _):
         bulk(k).wait_send()
-        add(k).wait_send()
         return 0
 
     def back_sent(k, _):
@@ -383,21 +399,20 @@
         pltpu.VMEM((Y, CAP, N, BLK), f32),
         pltpu.VMEM((Y, N * CAP, BLK), f32),
         pltpu.VMEM((Y, N * CAP, BLK), f32),
-        pltpu.VMEM((2, 8, LANES), f32),
-        pltpu.VMEM((N, 8, LANES), f32),
+        pltpu.VMEM((3, 8, LANES), f32),
+        pltpu.VMEM((XC, 8, LANES), f32),
+        pltpu.VMEM((Z, 8, LANES), f32),
         pltpu.VMEM((Y, 8, LANES), f32),
         DMA((N,)),
         DMA((N,)),
         DMA((R,)),
         DMA((R,)),
-        DMA((N,)),
-        DMA((N,)),
         DMA((4, Y)),
         DMA((4, Y)),
-        DMA((3, XC)),
-        DMA((3, XC)),
-        DMA((2, Z)),
-        DMA((2, Z)),
+        DMA((4, XC)),
+        DMA((4, XC)),
+        DMA((3, Z)),
+        DMA((3, Z)),
         DMA((2,)),
         DMA,
         DMA((slots,)),
@@ -419,7 +434,7 @@
     )(features.reshape(NB, BLK, D), neg_blocks, w_in, w_out, own)
     loss = sums[0, 0] / sums[0, 1]
     shape = (1, 1, N, CAP, BLK)
-    return pos.reshape(shape), neg.reshape(shape), loss
+    return (pos * scale).reshape(shape), (neg * (1.0 / BLK)).reshape(shape), loss
 
 
 def solution(mesh):

time: 146 us -> 136 us (0.932)
  Pallas kernels: 137 us -> 127 us
  local copies, waits for them, and re-layouts: 4.94 us -> 2.01 us
  other arithmetic: 1.45 us -> 2.98 us
    pallas_call x1, Pallas kernels: 137 us -> 127 us  [step(): pl.pallas_call(functools.partial(kernel, dims, scale), in_specs=[pl.Block...]
    unnamed x2 -> x0, local copies, waits for them, and re-layouts: 2.95 us -> none
    mul x0 -> x1, other arithmetic: none -> 1.53 us  [step(): neg * (1.0 / BLK)]
where the time goes in v4:
time: 136 us; the launch traced here: 135 us
  Pallas kernels  127 us (93%)
  between operations  3.11 us (2%)
  other arithmetic  2.98 us (2%)
  local copies, waits for them, and re-layouts  2.01 us (1%)
    pallas_call x1, Pallas kernels, step(): pl.pallas_call(functools.partial(kernel, dims, scale), in_specs=[pl.Block...  127 us

profile of v4, /device:TPU:1, one launch (start us, length us, event | category | flops | bytes accessed | tf_op | source)
XLA Modules:
  0.0 134.8 jit_solution(7729921980517892304)
XLA Ops:
  0.6 0.7 compare_select_fusion
  1.3 0.8 pad_add_fusion
  2.1 0.7 reshape.78.own
  2.7 126.7 %step.1 = (f32[128,128]{1,0:T(8,128)}, f32[128,128]{1,0:T(8,128)}, f32[8,128]{1,0:T(8,128)}) custom-call(bf16[160,128,256]{2,1,0:T(8,128)(2,1)} %bitcast.13, s32[1,2]{1,0:T(1,128)} %chosen.1, bf16[256,256]{1,0:T(8,128)(2,1)} %w_in.1, bf16[256,256]{1,0:T(8,128)(2,1)} %w_out.1, s32[2,2,128]{2,1,0:T(2,128)} %reshape.78.own), custom_call_target="tpu_custom_call" | custom-call | tf_op jit(solution)/shard_map/step/pallas_call | solution.py:420
  129.5 1.3 fusion
  132.1 1.5 %broadcast_multiply_fusion = (f32[128,128]{1,0:T(8,128)}, f32[128,128]{1,0:T(8,128)}) fusion(f32[128,128]{1,0:T(8,128)} %get-tuple-element.7, f32[128,128]{1,0:T(8,128)} %get-tuple-element.6), kind=kLoop, calls=%fused_computation | loop fusion | flops 32768 | bytes 262144 | tf_op jit(solution)/shard_map/mul | solution.py:437
  (1 shorter events, 0.0 us)

commit v5 on v4

--- a/solution.py
+++ b/solution.py
@@ -206,8 +206,8 @@
     arrived(pool_c)
 
     def negatives(e, _):
-        for k in range(2 * CAP):
-            r, o = e >> bits(N // 2), (e & (N // 2 - 1)) * 2 + k // CAP
+        for k in range(4 * CAP):
+            r, o = e >> bits(N // 4), (e & (N // 4 - 1)) * 4 + k // CAP
             s = near_s[0, r * CAP + k % CAP, o]
             p = near_s[1, r * CAP + k % CAP, o]
             node = p >> bits(NEG)
@@ -224,7 +224,7 @@
             negp[r, pl.ds(o * CAP + k % CAP, 1), :] = jnp.where(s >= 0, total, 0.0)
         return 0
 
-    lax.fori_loop(0, Y * N // 2, negatives, 0)
+    lax.fori_loop(0, Y * N // 4, negatives, 0)
     neg_y = start(y_stage(1, lambda to: negp.at[to], negr.at[q]))
 
     arrived(ids_c)
@@ -236,43 +236,62 @@
         t = jnp.swapaxes(jnp.concatenate([a] * (LANES // N), axis=0), 0, 1)[:N]
         idc[pl.ds(k, N, stride=RC), :] = jnp.where(lane < HALF, t, a)
 
-    number = lax.broadcasted_iota(jnp.int32, (2 * N * RC, NB), 1).astype(jnp.float32)
+    number = lax.broadcasted_iota(jnp.int32, (N * RC, LANES), 1).astype(jnp.float32)
 
     def gather(s):
-        cols = pltpu.roll(idc[...], (LANES - s) % LANES, 1)
-        col = jnp.concatenate([cols[:, :1], cols[:, HALF : HALF + 1]], axis=0)
-        hot = jnp.where(col == number, 1.0, 0.0).astype(jnp.bfloat16)
+        hots = []
+        for k in range(2):
+            at = jnp.full((N * RC, LANES), s + k * HALF, jnp.int32)
+            col = jnp.take_along_axis(idc[...], at, axis=1)
+            hot = [jnp.where(col == number, 1.0, 0.0).astype(jnp.bfloat16)]
+            if NB > LANES:
+                rest = jnp.where(col == number + LANES, 1.0, 0.0).astype(jnp.bfloat16)
+                hot.append(rest[:, : NB - LANES])
+            hots.append(jnp.concatenate(hot, axis=1)[:, :NB])
+        hot = jnp.concatenate(hots, axis=0)
         got = jnp.dot(hot, recv[s], preferred_element_type=jnp.float32).astype(jnp.bfloat16)
         ends[s] = got.reshape(2, N * RC, H)
 
+    def node_column(m):
+        return behind((m // C) * XC + m % C)
+
+    def node_others(m):
+        return behind((m // side) * XC + C + m % side)
+
     def gather_column(m, _):
-        column(m).wait_recv()
-        gather(behind((m // C) * XC + m % C))
+        for k in range(2):
+            column(2 * m + k).wait_recv()
+        for k in range(2):
+            gather(node_column(2 * m + k))
         return 0
 
     def gather_others(m, _):
-        others(m).wait_recv()
-        gather(behind((m // side) * XC + C + m % side))
-        return 0
-
+        for k in range(2):
+            others(2 * m + k).wait_recv()
+        for k in range(2):
+            gather(node_others(2 * m + k))
+        return 0
+
+    column(1).wait_recv()
     gather(me)
-    lax.fori_loop(1, Z * C, gather_column, 0)
-    lax.fori_loop(0, Z * side, gather_others, 0)
+    gather(node_column(1))
+    lax.fori_loop(1, Z * C // 2, gather_column, 0)
+    lax.fori_loop(0, Z * side // 2, gather_others, 0)
 
     shape = (N, RC, LANES)
     keep = lax.broadcasted_iota(jnp.int32, shape, 0) == lax.broadcasted_iota(jnp.int32, shape, 2)
 
     def dots(h, _):
-        at = pl.multiple_of(h * 2 * RC, 2 * RC)
-        b = ends[:, 1, pl.ds(at, 2 * RC), :].astype(jnp.float32)
-        for k in range(2):
-            i = 2 * h + k
+        at = pl.multiple_of(h * 4 * RC, 4 * RC)
+        b = ends[:, 1, pl.ds(at, 4 * RC), :].astype(jnp.float32)
+        for k in range(4):
+            i = 4 * h + k
             a = ends[i, 0].astype(jnp.float32).reshape(N, RC, H)
             sums = jnp.sum(a * b[:, k * RC : (k + 1) * RC], axis=2, keepdims=True)
             part[i // XC, (i % XC) // C, i % C] = jnp.sum(jnp.where(keep, sums, 0.0), axis=0)
         return 0
 
-    lax.fori_loop(0, N // 2, dots, 0)
+    lax.fori_loop(0, N // 4, dots, 0)
 
     to = z * XC + x * C + (c + 1) % C
     swap = copy(part.at[:, :, (c + 1) % C], other, die.at[0], die.at[1], to, q)

time: 136 us -> 120 us (0.88)
  Pallas kernels: 127 us -> 112 us
    pallas_call x1, Pallas kernels: 127 us -> 112 us  [step(): pl.pallas_call(functools.partial(kernel, dims, scale), in_specs=[pl.Block...]
where the time goes in v5:
time: 120 us
  Pallas kernels  112 us (93%)
  between operations  3.11 us (3%)
  other arithmetic  2.98 us (2%)
  local copies, waits for them, and re-layouts  2.01 us (2%)
    pallas_call x1, Pallas kernels, step(): pl.pallas_call(functools.partial(kernel, dims, scale), in_specs=[pl.Block...  112 us

profile of v5, /device:TPU:1, one launch (start us, length us, event | category | flops | bytes accessed | tf_op | source)
XLA Modules:
  0.0 119.8 jit_solution(1282770801225509315)
XLA Ops:
  0.6 0.7 compare_select_fusion
  1.3 0.8 pad_add_fusion
  2.1 0.7 reshape.78.own
  2.7 111.7 %step.1 = (f32[128,128]{1,0:T(8,128)}, f32[128,128]{1,0:T(8,128)}, f32[8,128]{1,0:T(8,128)}) custom-call(bf16[160,128,256]{2,1,0:T(8,128)(2,1)} %bitcast.13, s32[1,2]{1,0:T(1,128)} %chosen.1, bf16[256,256]{1,0:T(8,128)(2,1)} %w_in.1, bf16[256,256]{1,0:T(8,128)(2,1)} %w_out.1, s32[2,2,128]{2,1,0:T(2,128)} %reshape.78.own), custom_call_target="tpu_custom_call" | custom-call | tf_op jit(solution)/shard_map/step/pallas_call | solution.py:439
  114.5 1.3 %fusion = (f32[1,1]{1,0:T(1,128)}, f32[1,1]{1,0:T(1,128)}) fusion(f32[8,128]{1,0:T(8,128)} %get-tuple-element.8), kind=kLoop, calls=%fused_computation.5 | loop fusion | bytes 16 | tf_op jit(solution)/shard_map/slice | solution.py:454
  117.2 1.5 %broadcast_multiply_fusion = (f32[128,128]{1,0:T(8,128)}, f32[128,128]{1,0:T(8,128)}) fusion(f32[128,128]{1,0:T(8,128)} %get-tuple-element.7, f32[128,128]{1,0:T(8,128)} %get-tuple-element.6), kind=kLoop, calls=%fused_computation | loop fusion | flops 32768 | bytes 262144 | tf_op jit(solution)/shard_map/mul | solution.py:456
  (1 shorter events, 0.0 us)

commit v6 on v5

--- a/solution.py
+++ b/solution.py
@@ -23,7 +23,7 @@
 
 
 def kernel(
-    dims, scale, feat, chosen, w_in, w_out, own, pos_out, neg_out, loss_out,
+    dims, scale, feat, chosen, w_in, w_out, src, dst, picked, counts, pos_out, neg_out, loss_out,
     xq, stage, emb, send, recv, pool, near, ids, idc, near_v, near_s, ends, part, other, half, ret, tall, ysend, yrecv,
     negp, negr, tot, lc, lz, ly,
     bulk_s, bulk_r, back_s, back_r, y_s, y_r, c_s, c_r, z_s, z_r, die, local, chunk_sem,
@@ -116,7 +116,14 @@
 
     tall[...] = jnp.zeros_like(tall)
     fill = lax.broadcasted_iota(jnp.int32, (2, RC, LANES), 1) // CAP == q
-    near_v[...] = jnp.where(fill, jnp.concatenate([own[...]] * Y, axis=1), 0)
+    alive = lax.broadcasted_iota(jnp.int32, (CAP, N), 0) < counts[...]
+
+    def pair(a, b):
+        gap = [] if N == HALF else [jnp.zeros((CAP, HALF - N), jnp.int32)]
+        return jnp.concatenate([a] + gap + [b] + gap, axis=1)
+
+    own = jnp.stack([pair(jnp.where(alive, src[...], -1), dst[...]), pair(picked[...], picked[...])])
+    near_v[...] = jnp.where(fill, jnp.concatenate([own] * Y, axis=1), 0)
     mine.wait()
     offer = jnp.concatenate([xq[chosen[0, k]] for k in range(NEG)], axis=0)
     pool[z, x, c] = encode(offer).reshape(NEG, R, D)
@@ -144,13 +151,16 @@
         to = ahead(k)
         return copy(send.at[to // C, to % C], recv.at[me], bulk_s.at[k], bulk_r.at[k], to, q)
 
+    def turn(i):
+        return jnp.where(i % 2 == 1, (i + 1) // 2, (Z - i // 2) % Z)
+
     def column(m):
-        return bulk((m // C) * XC + m % C)
+        return bulk(turn(m // C) * XC + m % C)
 
     side = (X - 1) * C
 
     def others(m):
-        return bulk((m // side) * XC + C + m % side)
+        return bulk(turn(m // side) * XC + C + m % side)
 
     def column_go(m, _):
         column(m).start()
@@ -253,10 +263,10 @@
         ends[s] = got.reshape(2, N * RC, H)
 
     def node_column(m):
-        return behind((m // C) * XC + m % C)
+        return behind(turn(m // C) * XC + m % C)
 
     def node_others(m):
-        return behind((m // side) * XC + C + m % side)
+        return behind(turn(m // side) * XC + C + m % side)
 
     def gather_column(m, _):
         for k in range(2):
@@ -302,8 +312,7 @@
         neg = neg + negr[(q + j) % Y]
     neg_out[...] = neg
     loss = jnp.sum(neg) * (1.0 / BLK)
-    edge = lax.broadcasted_iota(jnp.int32, (CAP, LANES), 1) < N
-    count = jnp.sum(jnp.where(edge & (own[0] >= 0), 1.0, 0.0)) * BLK
+    count = jnp.sum(jnp.where(alive, 1.0, 0.0)) * BLK
     swap.wait_recv()
     v = part[:, :, c] + other[...]
     half[...] = v
@@ -390,11 +399,7 @@
     NEG = neg_blocks.shape[1]
     bf, f32, i32 = jnp.bfloat16, jnp.float32, jnp.int32
     scale = 1.0 / D**0.5
-    src, dst, pick = (t.reshape(N, CAP) for t in (pos_src, pos_dst, neg_pick))
-    live = jnp.arange(CAP, dtype=i32)[None, :] < counts.reshape(N, 1)
-    own = jnp.stack([jnp.where(live, src, -1), dst, pick, pick])
-    own = jnp.transpose(own.reshape(2, 2, N, CAP), (0, 3, 1, 2))
-    own = jnp.pad(own, ((0, 0), (0, 0), (0, 0), (0, HALF - N))).reshape(2, CAP, LANES)
+    src, dst, pick = (t.reshape(N, CAP).T for t in (pos_src, pos_dst, neg_pick))
     per, slots = (8, 4) if NB % 8 == 0 else (NB, 1)
     scratch = [
         pltpu.VMEM((NB, R, D), bf),
@@ -438,7 +443,7 @@
     ]
     pos, neg, sums = pl.pallas_call(
         functools.partial(kernel, dims, scale),
-        in_specs=[pl.BlockSpec(memory_space=pl.ANY), pl.BlockSpec(memory_space=pltpu.SMEM)] + [VMEM] * 3,
+        in_specs=[pl.BlockSpec(memory_space=pl.ANY), pl.BlockSpec(memory_space=pltpu.SMEM)] + [VMEM] * 6,
         out_specs=[VMEM] * 3,
         out_shape=[
             jax.ShapeDtypeStruct((N * CAP, BLK), f32),
@@ -450,7 +455,7 @@
             collective_id=0, has_side_effects=True, vmem_limit_bytes=60 * 2**20
         ),
         name="step",
-    )(features.reshape(NB, BLK, D), neg_blocks, w_in, w_out, own)
+    )(features.reshape(NB, BLK, D), neg_blocks, w_in, w_out, src, dst, pick, counts.reshape(1, N))
     loss = sums[0, 0] / sums[0, 1]
     shape = (1, 1, N, CAP, BLK)
     return (pos * scale).reshape(shape), (neg * (1.0 / BLK)).reshape(shape), loss

time: 120 us -> 114 us (0.950)
  Pallas kernels: 112 us -> 107 us
  other arithmetic: 2.98 us -> 1.53 us
    pallas_call x1, Pallas kernels: 112 us -> 107 us  [step(): pl.pallas_call(functools.partial(kernel, dims, scale), in_specs=[pl.Block...]
where the time goes in v6:
time: 114 us; the launch traced here: 113 us
  Pallas kernels  107 us (94%)
  between operations  3.11 us (3%)
  other arithmetic  1.53 us (1%)
  local copies, waits for them, and re-layouts  1.34 us (1%)
    pallas_call x1, Pallas kernels, step(): pl.pallas_call(functools.partial(kernel, dims, scale), in_specs=[pl.Block...  107 us

profile of v6, /device:TPU:1, one launch (start us, length us, event | category | flops | bytes accessed | tf_op | source)
XLA Modules:
  0.0 112.7 jit_solution(14480747814703146006)
XLA Ops:
  0.6 106.7 %step.1 = (f32[128,128]{1,0:T(8,128)}, f32[128,128]{1,0:T(8,128)}, f32[8,128]{1,0:T(8,128)}) custom-call(bf16[160,128,256]{2,1,0:T(8,128)(2,1)} %bitcast.14, s32[1,2]{1,0:T(1,128)} %chosen.1, bf16[256,256]{1,0:T(8,128)(2,1)} %w_in.1, bf16[256,256]{1,0:T(8,128)(2,1)} %w_out.1, s32[2,64]{1,0:T(2,128)} %bitcast.17, s32[2,64]{1,0:T(2,128)} %bitcast.18, ...), custom_call_target="tpu_custom_call" | custom-call | tf_op jit(solution)/shard_map/step/pallas_call | solution.py:444
  107.3 1.3 %fusion = (f32[1,1]{1,0:T(1,128)}, f32[1,1]{1,0:T(1,128)}) fusion(f32[8,128]{1,0:T(8,128)} %get-tuple-element.8), kind=kLoop, calls=%fused_computation.2 | loop fusion | bytes 16 | tf_op jit(solution)/shard_map/slice | solution.py:459
  110.0 1.5 %broadcast_multiply_fusion = (f32[128,128]{1,0:T(8,128)}, f32[128,128]{1,0:T(8,128)}) fusion(f32[128,128]{1,0:T(8,128)} %get-tuple-element.7, f32[128,128]{1,0:T(8,128)} %get-tuple-element.6), kind=kLoop, calls=%fused_computation | loop fusion | flops 32768 | bytes 262144 | tf_op jit(solution)/shard_map/mul | solution.py:461

commit v7 on v6

--- a/solution.py
+++ b/solution.py
@@ -276,17 +276,17 @@
         return 0
 
     def gather_others(m, _):
-        for k in range(2):
-            others(2 * m + k).wait_recv()
-        for k in range(2):
-            gather(node_others(2 * m + k))
+        for k in range(4):
+            others(4 * m + k).wait_recv()
+        for k in range(4):
+            gather(node_others(4 * m + k))
         return 0
 
     column(1).wait_recv()
     gather(me)
     gather(node_column(1))
     lax.fori_loop(1, Z * C // 2, gather_column, 0)
-    lax.fori_loop(0, Z * side // 2, gather_others, 0)
+    lax.fori_loop(0, Z * side // 4, gather_others, 0)
 
     shape = (N, RC, LANES)
     keep = lax.broadcasted_iota(jnp.int32, shape, 0) == lax.broadcasted_iota(jnp.int32, shape, 2)

time: 114 us -> 114 us (level)
  no operation moved by 1% of the time
where the time goes in v7:
time: 114 us; the launch traced here: 112 us
  Pallas kernels  106 us (93%)
  between operations  3.11 us (3%)
  other arithmetic  1.53 us (1%)
  local copies, waits for them, and re-layouts  1.34 us (1%)
    pallas_call x1, Pallas kernels, step(): pl.pallas_call(functools.partial(kernel, dims, scale), in_specs=[pl.Block...  106 us

profile of v7, /device:TPU:1, one launch (start us, length us, event | category | flops | bytes accessed | tf_op | source)
XLA Modules:
  0.0 112.4 jit_solution(17145742736229216741)
XLA Ops:
  0.6 106.4 %step.1 = (f32[128,128]{1,0:T(8,128)}, f32[128,128]{1,0:T(8,128)}, f32[8,128]{1,0:T(8,128)}) custom-call(bf16[160,128,256]{2,1,0:T(8,128)(2,1)} %bitcast.14, s32[1,2]{1,0:T(1,128)} %chosen.1, bf16[256,256]{1,0:T(8,128)(2,1)} %w_in.1, bf16[256,256]{1,0:T(8,128)(2,1)} %w_out.1, s32[2,64]{1,0:T(2,128)} %bitcast.17, s32[2,64]{1,0:T(2,128)} %bitcast.18, ...), custom_call_target="tpu_custom_call" | custom-call | tf_op jit(solution)/shard_map/step/pallas_call | solution.py:444
  107.1 1.3 %fusion = (f32[1,1]{1,0:T(1,128)}, f32[1,1]{1,0:T(1,128)}) fusion(f32[8,128]{1,0:T(8,128)} %get-tuple-element.8), kind=kLoop, calls=%fused_computation.2 | loop fusion | bytes 16 | tf_op jit(solution)/shard_map/slice | solution.py:459
  109.7 1.5 %broadcast_multiply_fusion = (f32[128,128]{1,0:T(8,128)}, f32[128,128]{1,0:T(8,128)}) fusion(f32[128,128]{1,0:T(8,128)} %get-tuple-element.7, f32[128,128]{1,0:T(8,128)} %get-tuple-element.6), kind=kLoop, calls=%fused_computation | loop fusion | flops 32768 | bytes 262144 | tf_op jit(solution)/shard_map/mul | solution.py:461
